TPU v7x, 32 devices: a whole 2x2x4 slice. The times are simulated.
32 devices in a mesh: gx: 4 (over x, core), gy: 4 (over z), gz: 2 (over y).
Axes of the slice: x: 2, y: 2, z: 4, core: 2. Of those that a mesh axis runs over, the one named last changes fastest.
Arguments:
- chemical_log_concentrations: float32 [53, 12, 96, 256], P(None, 'gx', 'gy', 'gz'), may hold values from -6 to 6
- advection_wind: float32 [3, 12, 96, 256], P(None, 'gx', 'gy', 'gz'), may hold values from -1 to 1
- inverse_thermal_scale: float32 [12, 96, 256], P('gx', 'gy', 'gz'), may hold values from 0.3 to 1.2
- kinetics_column_switch: int32 [1, 12, 96, 2], P(None, 'gx', 'gy', 'gz'), may hold values from 0 to 1, as said below
- kinetic_exponents: bfloat16 [192, 53], replicated, may hold values from -0.875 to 0.875
- arrhenius_log_coefficient: float32 [192], replicated, may hold values from -2 to 0
- arrhenius_energy: float32 [192], replicated, may hold values from 0.5 to 4
- stoichiometric_production: bfloat16 [53, 192], replicated, may hold values from -0.4375 to 0.4375
- formation_heat: float32 [53], replicated, may hold values from -0.875 to 0.875
- streamwise_tucker_basis: float32 [12, 64], P('gx'), may hold values from -1.75 to 1.75
Outputs:
- species_out: float32 [53, 12, 96, 256], P(None, 'gx', 'gy', 'gz')
- core: float32 [4, 64, 24, 256], P('gy', None, 'gx', 'gz')
Inputs may be any that keep to these rules, and one draw needn't show every extreme that they name: `kinetics_column_switch`: A pencil is the 128 cells along z of one device at one x and y. In each evaluation the 8 devices that share an index of gx hold exactly 128 hot pencils together, no device holds more than 64, and one of them holds exactly 64.
All inputs are finite; a program needn't handle non-finite values.
Results may differ from a plain program's by a relative error of at most 0.0065.
Values may be sent and summed in bfloat16 or wider, within the bound.
No kernel may reach another device: no remote copies, remote signals or barrier semaphores. Data moves between devices by JAX's collectives and lax.ppermute only.
A program may use at most 128 MiB of HBM per device.

v0:
```python
import jax
import jax.numpy as jnp
from jax import lax
from jax.experimental import pallas as pl
from jax.experimental.pallas import tpu as pltpu
from jax.sharding import PartitionSpec as P

SUBSTEPS = 2
OCTET = 8
LANES = 128

flow_step = 0.15
sub_step = 0.04
smooth_eps = 1e-06


def shift(array, axis, by):
    count = lax.axis_size(axis)
    return lax.ppermute(array, axis, [(i, (i + by) % count) for i in range(count)])


def swap(array, axis, late):
    count = lax.axis_size(axis)
    pairs = [(i, (i + 1) % count) for i in range(late, count + late, 2)]
    pairs = [(a % count, b % count) for a, b in pairs]
    return lax.ppermute(array, axis, pairs + [(b, a) for a, b in pairs])


def close(array):
    return pltpu.with_memory_space_constraint(array, pltpu.VMEM)


def far(array):
    return pltpu.with_memory_space_constraint(array, pltpu.HBM)


def indicators(before, after):
    curve = after - before
    bent = 1.5 * curve
    centre = (curve * curve + 0.75 * smooth_eps) + 0.75 * (before * after)
    return centre + after * bent, centre, centre - before * bent


def faces(left, middle, right, third_low, third_high):
    ml = middle * left
    mr = middle * right
    lr = left * right
    ml = ml * ml
    mr = mr * mr
    lr = lr * lr
    total = (ml + mr) + 6.0 * lr
    first = ml * third_high
    second = mr * third_low
    both = 2.0 * (first + second)
    return (both + first) / (total + 2.0 * ml), (both + second) / (total + 2.0 * mr)


def line(load, count, speed, put):
    def kept(function):
        known = {}

        def get(i):
            if i not in known:
                known[i] = function(i)
            return known[i]

        return get

    u = kept(load)
    d = kept(lambda i: u(i + 1) - u(i))
    second = kept(lambda i: d(i) - d(i - 1))
    third = kept(lambda i: second(i) - second(i - 1))
    ind = kept(lambda i: indicators(d(i - 1), d(i)))
    both = kept(
        lambda i: faces(ind(i - 1)[0], ind(i)[1], ind(i + 1)[2], third(i), third(i + 1))
    )
    for i in range(count):
        v = speed(i)
        bend = jnp.where(
            v > 0.0,
            third(i) + (both(i)[0] - both(i - 1)[0]),
            third(i + 1) - (both(i + 1)[1] - both(i)[1]),
        )
        put(i, v * (3.0 * (d(i) + d(i - 1)) - bend))


def groups_of(species):
    return list(range(0, species - OCTET, OCTET)) + [species - OCTET]


def rounded(array):
    return array.astype(jnp.bfloat16).astype(jnp.float32)


def split_three(array):
    first = rounded(array)
    second = rounded(array - first)
    return [first, second, rounded(array - first - second)]


def prep_kernel(
    spot_ref, u_ref, *refs,
    species, width_x, width_y, row_tiles, spans,
):
    sources, refs = refs[:7], refs[7:]
    chunk_refs, refs = refs[: len(spans)], refs[len(spans) :]
    early_ref, late_ref, zpack_ref, order_ref, net_ref, heat_ref, wind_ref, scale_ref = refs[:8]
    zwide_ref, orders_ref, log_ref, energy_ref, net_in_ref, heat_in_ref, sems = refs[8:]
    targets = (wind_ref, scale_ref, orders_ref, log_ref, energy_ref, net_in_ref, heat_in_ref)
    copies = [
        pltpu.make_async_copy(source, target, sems.at[i])
        for i, (source, target) in enumerate(zip(sources, targets))
    ]
    for copy in copies:
        copy.start()
    pencils = width_x * width_y
    for c, (y0, y1) in enumerate(spans):
        for x in range(width_x):
            chunk_refs[c][:, x] = u_ref[
                :, x * width_y + y0 : x * width_y + y1, :
            ].astype(jnp.bfloat16)
    flat = u_ref.reshape(species * pencils, LANES)
    odd = lax.rem(spot_ref[0], 2)
    for g, s0 in enumerate(groups_of(species)):
        for x in range(width_x):
            for k in range(3):
                at = s0 * pencils + x * width_y + k
                shown = (x * 3 + k, slice(g * OCTET, (g + 1) * OCTET))
                early_ref[shown] = flat[
                    pl.ds(at + (1 - odd) * (width_y - 3), OCTET, stride=pencils), :
                ].astype(jnp.bfloat16)
                late_ref[shown] = flat[
                    pl.ds(at + odd * (width_y - 3), OCTET, stride=pencils), :
                ].astype(jnp.bfloat16)
    k = lax.broadcasted_iota(jnp.int32, (OCTET, LANES), 0)
    z = lax.broadcasted_iota(jnp.int32, (OCTET, LANES), 1)
    pick = jnp.where(
        ((k < 3) & (z == k)) | ((k >= 3) & (k < 6) & (z == LANES - 6 + k)), 1.0, 0.0
    ).astype(jnp.bfloat16)
    rows = species * pencils
    slots = zpack_ref.shape[0] // 6
    zwide_ref[...] = jnp.zeros(zwide_ref.shape, jnp.float32)
    for j in range(row_tiles):
        j0 = min(j * LANES, rows - LANES)
        block = flat[j0 : j0 + LANES, :].astype(jnp.bfloat16)
        ends = lax.dot_general(
            pick, block, (((1,), (1,)), ((), ())), preferred_element_type=jnp.float32
        )
        zwide_ref[pl.ds(j, OCTET, stride=slots), :] = ends
    zpack_ref[...] = zwide_ref[: 6 * slots, :].astype(jnp.bfloat16)

    for copy in copies:
        copy.wait()
    reactions, wide = order_ref.shape
    row = lax.broadcasted_iota(jnp.int32, (species, wide), 0)
    col = lax.broadcasted_iota(jnp.int32, (species, wide), 1)
    same = jnp.where(row == col, 1.0, 0.0).astype(jnp.bfloat16)
    bias = split_three(-energy_ref[...]) + split_three(log_ref[...])
    bias = jnp.concatenate(bias + [jnp.zeros((2, reactions), jnp.float32)], axis=0)
    row = lax.broadcasted_iota(jnp.int32, (OCTET, wide), 0)
    col = lax.broadcasted_iota(jnp.int32, (OCTET, wide), 1)
    late = jnp.where(col == wide - OCTET + row, 1.0, 0.0).astype(jnp.bfloat16)
    order_ref[...] = (
        lax.dot_general(
            orders_ref[...], same, (((0,), (0,)), ((), ())), preferred_element_type=jnp.float32
        )
        + lax.dot_general(
            bias.astype(jnp.bfloat16), late, (((0,), (0,)), ((), ())),
            preferred_element_type=jnp.float32,
        )
    ).astype(jnp.bfloat16)
    row = lax.broadcasted_iota(jnp.int32, (wide, species), 0)
    col = lax.broadcasted_iota(jnp.int32, (wide, species), 1)
    same = jnp.where(row == col, 1.0, 0.0).astype(jnp.bfloat16)
    net_ref[...] = jnp.dot(
        same, net_in_ref[...], preferred_element_type=jnp.float32
    ).astype(jnp.bfloat16)
    heats = split_three(-heat_in_ref[...])
    heats = jnp.concatenate(heats + [jnp.zeros((5, species), jnp.float32)], axis=0)
    heat_ref[...] = lax.dot_general(
        heats.astype(jnp.bfloat16), same, (((1,), (1,)), ((), ())),
        preferred_element_type=jnp.float32,
    ).astype(jnp.bfloat16)


def upward_kernel(
    u_ref, zlow_ref, zhigh_ref, v_ref, out_ref, across_ref, speed_ref, moved_ref,
    *, species, pencils, row_tiles, slots, pitch,
):
    rows = species * pencils
    flat = u_ref.reshape(rows, LANES)

    def first_row(j):
        return min(j * LANES, rows - LANES)

    for j in range(row_tiles, slots):
        across_ref[j * pitch : (j + 1) * pitch, :] = jnp.zeros((pitch, LANES), jnp.float32)
        speed_ref[j * pitch : (j + 1) * pitch, :] = jnp.zeros((pitch, LANES), jnp.float32)
    wind = v_ref[2]
    turned = {}
    for j in range(row_tiles):
        p0 = first_row(j) % pencils
        if p0 not in turned:
            strips, need, at = [], LANES, p0
            while need > 0:
                take = min(need, pencils - at)
                strips.append(wind[at : at + take])
                need, at = need - take, 0
            turned[p0] = jnp.concatenate(strips, axis=0).T
    for j in range(row_tiles):
        speed_ref[j * pitch : j * pitch + LANES, :] = turned[first_row(j) % pencils]
    for j in range(row_tiles):
        j0 = first_row(j)
        across_ref[j * pitch : j * pitch + LANES, :] = flat[j0 : j0 + LANES, :].T

    def upward(q, carry):
        t0 = pl.multiple_of(q * OCTET, OCTET)
        base = t0 * pitch

        def load(i):
            if i < 0:
                return zlow_ref[pl.ds((i + 6) * slots + t0, OCTET), :].astype(jnp.float32)
            if i >= LANES:
                return zhigh_ref[pl.ds((i - LANES) * slots + t0, OCTET), :].astype(jnp.float32)
            return across_ref[pl.ds(base + i, OCTET, stride=pitch), :]

        def speed(i):
            return speed_ref[pl.ds(base + i, OCTET, stride=pitch), :]

        def put(i, value):
            moved_ref[pl.ds(base + i, OCTET, stride=pitch), :] = value

        line(load, LANES, speed, put)
        return carry

    lax.fori_loop(0, slots // OCTET, upward, 0)

    for j in range(row_tiles):
        j0 = j * LANES
        size = min(LANES, rows - j0)
        skip = j0 - first_row(j)
        out_ref[j0 : j0 + size, :] = moved_ref[j * pitch : j * pitch + LANES, :].T[skip:]


def north_kernel(
    spot_ref, u_ref, z_ref, early_ref, late_ref, v_ref, out_ref, acc_ref,
    *, species, width_x, width_y,
):
    pencils = width_x * width_y
    rows = species * pencils
    flat = u_ref.reshape(rows, LANES)
    count = len(groups_of(species))
    odd = lax.rem(spot_ref[0], 2) == 1

    def north(step, carry):
        g = step // width_x
        x = step % width_x
        s0 = jnp.minimum(g * OCTET, species - OCTET)
        base = s0 * pencils + x * width_y
        g0 = pl.multiple_of(g * OCTET, OCTET)

        def load(i):
            if i < 0 or i >= width_y:
                at = (x * 3 + (i + 3 if i < 0 else i - width_y), pl.ds(g0, OCTET))
                ours, other = early_ref[at], late_ref[at]
                if i >= width_y:
                    ours, other = other, ours
                return jnp.where(odd, ours.astype(jnp.float32), other.astype(jnp.float32))
            return flat[pl.ds(base + i, OCTET, stride=pencils), :]

        def speed(i):
            return jnp.broadcast_to(v_ref[1, pl.ds(x * width_y + i, 1), :], (OCTET, LANES))

        def put(i, value):
            acc_ref[pl.ds(base + i, OCTET, stride=pencils), :] = value

        line(load, width_y, speed, put)
        return carry

    lax.fori_loop(0, count * width_x, north, 0)

    def close_up(s, carry):
        at = pl.ds(pl.multiple_of(s * pencils, OCTET), pencils)
        out_ref[at, :] = flat[at, :] - (flow_step / 6.0) * (acc_ref[at, :] + z_ref[at, :])
        return carry

    lax.fori_loop(0, species, close_up, 0)


def chunk_kernel(
    me_ref, hot_ref, u_ref, part_ref, early_ref, late_ref, wind_ref, scale_ref,
    order_ref, net_ref, heat_ref, basis_ref, *refs,
    species, width_x, span, members, share, first, last,
):
    refs = list(refs)
    before_ref = None
    if not first:
        before_ref = refs.pop(0)
        refs.pop(0)
    out_hbm = refs.pop(0)
    out_ref, cells_ref, out_sems = refs[-3:]
    refs = refs[:-3]
    release_ref = refs.pop() if last else refs.pop(0)
    y0, y1 = span
    width = y1 - y0
    octets = width // OCTET
    together = 2 if octets == 1 else 1
    odd = lax.rem(me_ref[0], 2)
    width_y = scale_ref.shape[1]
    u_ref = u_ref.reshape(species, width_x, width_y, LANES)
    part_ref = part_ref.reshape(species, width_x, width_y, LANES)

    def east(s, low_ref, high_ref):
        for o in range(octets):
            at = slice(o * OCTET, (o + 1) * OCTET)
            there = slice(y0 + o * OCTET, y0 + (o + 1) * OCTET)

            def load(i):
                if i < 0:
                    return low_ref[s, i + width_x, at].astype(jnp.float32)
                if i >= width_x:
                    return high_ref[s, i - width_x, at].astype(jnp.float32)
                return u_ref[s, i, there]

            def put(i, value):
                out_ref[s, i, at] = part_ref[s, i, there] - (flow_step / 6.0) * value

            line(load, width_x, lambda i: wind_ref[0, i * width_y + there.start : i * width_y + there.stop], put)

    for parity, low_ref, high_ref in ((0, late_ref, early_ref), (1, early_ref, late_ref)):

        @pl.when(odd == parity)
        def _(low_ref=low_ref, high_ref=high_ref):
            def several(step, carry):
                for extra in range(together):
                    east(step * together + extra, low_ref, high_ref)
                return carry

            lax.fori_loop(0, species // together, several, 0)
            for rest in range(species // together * together, species):
                east(rest, low_ref, high_ref)

    if first:
        release_ref[...] = jnp.zeros(release_ref.shape, jnp.float32)
    else:
        release_ref[...] = before_ref[...]
    rows = width_x * width
    flat = out_ref.reshape(species * rows, LANES)
    starts = [(s0, min(OCTET, species - s0)) for s0 in range(0, species, OCTET)]
    sublane = lax.broadcasted_iota(jnp.int32, (OCTET, LANES), 0)
    order = order_ref[...]
    net = net_ref[...]
    heat = heat_ref[...]
    depth = order.shape[1]
    for block in range(width_x * octets):
        x, o = block // octets, block % octets
        for y in range(OCTET):
            cols = slice(y * LANES, (y + 1) * LANES)
            at = x * width + o * OCTET + y
            cells_ref[block, depth - 2 * OCTET : depth - OCTET, cols] = jnp.zeros(
                (OCTET, LANES), jnp.float32
            )
            for s0, size in starts:
                cells_ref[block, s0 : s0 + size, cols] = flat[
                    pl.ds(s0 * rows + at, size, stride=rows), :
                ]
            theta = jnp.broadcast_to(
                scale_ref[x, y0 + o * OCTET + y : y0 + o * OCTET + y + 1, :], (OCTET, LANES)
            )
            cells_ref[block, depth - OCTET :, cols] = jnp.where(
                sublane < 3, theta, jnp.where(sublane < 6, 1.0, 0.0)
            )
    stores = []
    for block in range(width_x * octets):
        x, o = block // octets, block % octets
        start = rounded(cells_ref[block])
        current = start
        for _ in range(SUBSTEPS):
            features = current.astype(jnp.bfloat16)
            exponent = jnp.dot(order, features, preferred_element_type=jnp.float32)
            rates = jnp.exp(exponent).astype(jnp.bfloat16)
            source = jnp.dot(net, rates, preferred_element_type=jnp.float32)
            current = current + sub_step * rounded(source)
        increment = rounded(current - start)
        for y in range(OCTET):
            cols = slice(y * LANES, (y + 1) * LANES)
            row = y0 + o * OCTET + y
            at = x * width + o * OCTET + y
            gain = jnp.where(hot_ref[x, 0, row] > 0, increment[:, cols], 0.0)
            for s0, size in starts:
                flat[pl.ds(s0 * rows + at, size, stride=rows), :] = (
                    cells_ref[block, s0 : s0 + size, cols] + gain[s0 : s0 + size, :]
                )
            sums = jnp.dot(heat, gain.astype(jnp.bfloat16), preferred_element_type=jnp.float32)
            release_ref[row // share, x, row % share : row % share + 1, :] = (
                sums[0:1] + sums[1:2] + sums[2:3]
            )
        if o == octets - 1:
            stores.append(
                pltpu.make_async_copy(
                    out_ref.at[:, x], out_hbm.at[:, x, pl.ds(y0, width)], out_sems.at[x]
                )
            )
            stores[-1].start()
    if last:
        modes = basis_ref.shape[1]
        for k in range(members):
            for x in range(width_x):
                release_ref[k, x, OCTET - 1 :, 0:modes] = basis_ref[x : x + 1, :]
        for j in range(members):
            refs[j][...] = release_ref[lax.rem(me_ref[0] + j, members)]
    for store in stores:
        store.wait()


def core_kernel(*refs, members, width_x, share, modes):
    parts = refs[:members]
    out_ref, rows_ref = refs[members:]
    lines = members * width_x
    padded = rows_ref.shape[0] // OCTET
    for j in range(members):
        for x in range(width_x):
            at = (j * width_x + x) * OCTET
            rows_ref[at : at + OCTET, :] = parts[j][x]
    if padded > lines:
        rows_ref[lines * OCTET :, :] = jnp.zeros(((padded - lines) * OCTET, LANES), jnp.float32)

    def gather(y):
        return jnp.concatenate(
            [
                rows_ref[pl.ds(a * OCTET * OCTET + y, OCTET, stride=OCTET), :]
                for a in range(padded // OCTET)
            ],
            axis=0,
        )

    basis = gather(OCTET - 1).T[:modes]
    for y in range(share):
        out_ref[y] = jnp.dot(
            basis, gather(y), preferred_element_type=jnp.float32, precision=lax.Precision.HIGHEST
        )


def body(
    chemical_log_concentrations,
    advection_wind,
    inverse_thermal_scale,
    kinetics_column_switch,
    kinetic_exponents,
    arrhenius_log_coefficient,
    arrhenius_energy,
    stoichiometric_production,
    formation_heat,
    streamwise_tucker_basis,
):
    species, width_x, width_y, depth = chemical_log_concentrations.shape
    pencils = width_x * width_y
    rows = species * pencils
    row_tiles = -(-rows // LANES)
    slots = -(-row_tiles // OCTET) * OCTET
    pitch = LANES + OCTET
    padded = len(groups_of(species)) * OCTET
    reactions = kinetic_exponents.shape[0]
    members = lax.axis_size("gx")
    share = width_y // members
    modes = streamwise_tucker_basis.shape[1]
    cut = width_y - OCTET
    spans = [(0, cut), (cut, width_y)]
    vmem = pl.BlockSpec(memory_space=pltpu.VMEM)
    smem = pl.BlockSpec(memory_space=pltpu.SMEM)
    flat_u = close(chemical_log_concentrations.reshape(species, pencils, depth))
    params = pltpu.CompilerParams(vmem_limit_bytes=32 * 1024 * 1024)

    def chunk(span):
        return jax.ShapeDtypeStruct((species, width_x, span[1] - span[0], LANES), jnp.bfloat16)

    side = jax.ShapeDtypeStruct((width_x * 3, padded, LANES), jnp.bfloat16)
    any_spec = pl.BlockSpec(memory_space=pl.ANY)
    me = lax.axis_index("gx").astype(jnp.int32).reshape(1)
    spot = lax.axis_index("gy").astype(jnp.int32).reshape(1)
    *chunks, y_early, y_late, z_own, order, net, heat, wind, scale = pl.pallas_call(
        lambda *refs: prep_kernel(
            *refs, species=species, width_x=width_x, width_y=width_y, row_tiles=row_tiles,
            spans=spans,
        ),
        in_specs=[smem, vmem] + [any_spec] * 7,
        out_specs=[vmem] * (len(spans) + 8),
        out_shape=[chunk(span) for span in spans]
        + [
            side,
            side,
            jax.ShapeDtypeStruct((6 * slots, LANES), jnp.bfloat16),
            jax.ShapeDtypeStruct((reactions, padded + OCTET), jnp.bfloat16),
            jax.ShapeDtypeStruct((padded + OCTET, reactions), jnp.bfloat16),
            jax.ShapeDtypeStruct((OCTET, padded + OCTET), jnp.bfloat16),
            pltpu.VMEM((3, pencils, depth), jnp.float32),
            pltpu.VMEM((width_x, width_y, depth), jnp.float32),
        ],
        scratch_shapes=[
            pltpu.VMEM((OCTET * slots, LANES), jnp.float32),
            pltpu.VMEM((species, reactions), jnp.bfloat16),
            pltpu.VMEM((1, reactions), jnp.float32),
            pltpu.VMEM((1, reactions), jnp.float32),
            pltpu.VMEM((species, reactions), jnp.bfloat16),
            pltpu.VMEM((1, species), jnp.float32),
            pltpu.SemaphoreType.DMA((7,)),
        ],
        compiler_params=params,
        name="prep",
    )(
        spot,
        flat_u,
        far(advection_wind.reshape(3, pencils, depth)),
        far(inverse_thermal_scale),
        far(kinetic_exponents.T),
        far(arrhenius_log_coefficient.reshape(1, reactions)),
        far(arrhenius_energy.reshape(1, reactions)),
        far(stoichiometric_production),
        far(formation_heat.reshape(1, species)),
    )

    z_low = shift(z_own, "gz", 1)
    z_high = z_low if lax.axis_size("gz") == 2 else shift(z_own, "gz", -1)
    x_late = [swap(chunks[0], "gx", 1)]
    late_rows = swap(y_late, "gy", 1)
    early_rows = swap(y_early, "gy", 0)
    x_early = [swap(part, "gx", 0) for part in chunks]
    x_late += [swap(part, "gx", 1) for part in chunks[1:]]

    cells = rows * depth
    raised = pl.pallas_call(
        lambda *refs: upward_kernel(
            *refs, species=species, pencils=pencils, row_tiles=row_tiles, slots=slots, pitch=pitch
        ),
        in_specs=[vmem] * 4,
        out_specs=vmem,
        out_shape=pltpu.VMEM((rows, depth), jnp.float32),
        scratch_shapes=[pltpu.VMEM((slots * pitch, LANES), jnp.float32)] * 3,
        cost_estimate=pl.CostEstimate(
            flops=cells * 60, bytes_accessed=cells * 8, transcendentals=cells * 2
        ),
        compiler_params=params,
        name="upward",
    )(flat_u, close(z_low), close(z_high), wind)
    part = pl.pallas_call(
        lambda *refs: north_kernel(*refs, species=species, width_x=width_x, width_y=width_y),
        in_specs=[smem] + [vmem] * 5,
        out_specs=vmem,
        out_shape=pltpu.VMEM((rows, depth), jnp.float32),
        scratch_shapes=[pltpu.VMEM((rows, LANES), jnp.float32)],
        cost_estimate=pl.CostEstimate(
            flops=cells * 60, bytes_accessed=cells * 8, transcendentals=cells * 2
        ),
        compiler_params=params,
        name="north",
    )(spot, flat_u, raised, close(early_rows), close(late_rows), wind)
    state = None

    hot = jnp.swapaxes(kinetics_column_switch, 2, 3).reshape(width_x, 1, width_y)
    release = None
    tile = jax.ShapeDtypeStruct((width_x, OCTET, LANES), jnp.float32)
    pile = jax.ShapeDtypeStruct((members, width_x, OCTET, LANES), jnp.float32)
    for c, span in enumerate(spans):
        width = span[1] - span[0]
        first, last = c == 0, c == len(spans) - 1

        outs = [tile] * members if last else [pile]
        results = pl.pallas_call(
            lambda *refs, first=first, last=last, span=span: chunk_kernel(
                *refs, species=species, width_x=width_x, span=span, members=members,
                share=share, first=first, last=last,
            ),
            in_specs=[smem, smem] + [vmem] * 10 + ([] if first else [vmem, any_spec]),
            out_specs=[any_spec] + [vmem] * len(outs),
            out_shape=[jax.ShapeDtypeStruct(chemical_log_concentrations.shape, jnp.float32)] + outs,
            scratch_shapes=([pltpu.VMEM(pile.shape, jnp.float32)] if last else [])
            + [
                pltpu.VMEM((species, width_x, width, LANES), jnp.float32),
                pltpu.VMEM(
                    (width_x * width // OCTET, padded + OCTET, OCTET * LANES), jnp.float32
                ),
                pltpu.SemaphoreType.DMA((width_x,)),
            ],
            input_output_aliases={} if first else {13: 0},
            compiler_params=params,
            cost_estimate=pl.CostEstimate(
                flops=cells * 60, bytes_accessed=cells * 4, transcendentals=cells * 4
            ),
        )(
            me, hot, flat_u, part, close(x_early[c]), close(x_late[c]), wind, scale, order, net, heat, streamwise_tucker_basis,
            *([] if first else [release, state]),
        )
        state = results[0]
        release = results[1]
    pieces = results[1:]

    moved = [pieces[0]] + [close(shift(pieces[j], "gx", j)) for j in range(1, members)]
    lines = -(-members * width_x // OCTET) * OCTET
    core = pl.pallas_call(
        lambda *refs: core_kernel(
            *refs, members=members, width_x=width_x, share=share, modes=modes
        ),
        in_specs=[vmem] * members,
        out_specs=vmem,
        out_shape=jax.ShapeDtypeStruct((share, modes, depth), jnp.float32),
        scratch_shapes=[pltpu.VMEM((lines * OCTET, LANES), jnp.float32)],
        compiler_params=params,
        name="core",
    )(*moved)
    return (state, core.transpose(1, 0, 2)[None])


def solution(mesh):
    placed = (
        P(None, "gx", "gy", "gz"),
        P(None, "gx", "gy", "gz"),
        P("gx", "gy", "gz"),
        P(None, "gx", "gy", "gz"),
        P(),
        P(),
        P(),
        P(),
        P(),
        P("gx", None),
    )
    return jax.shard_map(
        body,
        mesh=mesh,
        in_specs=placed,
        out_specs=(P(None, "gx", "gy", "gz"), P("gy", None, "gx", "gz")),
        check_vma=False,
    )
```

profile of v0, /device:TPU:0, one launch (start us, length us, event | category | flops | bytes accessed | tf_op | source)
XLA Modules:
  0.0 53.7 jit_solution(8935225826627914686)
XLA Ops:
  0.6 1.5 %copy-done = f32[53,3,24,128]{3,2,1,0:T(8,128)S(1)} copy-done((f32[53,3,24,128]{3,2,1,0:T(8,128)S(1)}, f32[53,3,24,128]{3,2,1,0:T(8,128)}, u32[]{:S(2)}) %copy-start) | copy-done | bytes 1953816
  2.2 2.3 %prep.1 = (bf16[53,3,16,128]{3,2,1,0:T(8,128)(2,1)}, bf16[53,3,8,128]{3,2,1,0:T(8,128)(2,1)}, bf16[9,56,128]{2,1,0:T(8,128)(2,1)S(1)}, bf16[9,56,128]{2,1,0:T(8,...) custom-call(s32[1]{0:T(128)} %bitcast.3.refs_0_, ...), custom_call_target="tpu_custom_call" | custom-call | tf_op jit(solution)/shard_map/prep/pallas_call | solution.py:481
  4.5 2.5 %collective-permute-start.6 = (bf16[53,3,16,128]{3,2,1,0:T(8,128)(2,1)}, bf16[53,3,16,128]{3,2,1,0:T(8,128)(2,1)S(1)}, u32[]{:S(2)}, u32[]{:S(2)}) collective-permute-start(bf16[53,3,16,128]{3,2,1,0:T(8,128)(2,1)} %get-tuple-element.28), channel_id=1, source_target_pairs={{8,16},{24,0},{16,8},{0,24},{9,17},{25,1},{17,9},{1,25},{10,18},{2... | collective-permute-start | bytes 1953800 | tf_op jit(solution)/shard_map/ppermute | solution.py:26
  7.0 0.7 %collective-permute-start.5 = (bf16[53,3,16,128]{3,2,1,0:T(8,128)(2,1)}, bf16[53,3,16,128]{3,2,1,0:T(8,128)(2,1)S(1)}, u32[]{:S(2)}, u32[]{:S(2)}) collective-permute-start(bf16[53,3,16,128]{3,2,1,0:T(8,128)(2,1)} %get-tuple-element.28), channel_id=1, source_target_pairs={{0,8},{16,24},{8,0},{24,16},{1,9},{17,25},{9,1},{25,17},{2,10},{18... | collective-permute-start | bytes 1953800 | tf_op jit(solution)/shard_map/ppermute | solution.py:26
  7.6 0.1 collective-permute-start.4
  7.7 0.1 collective-permute-start.3
  7.8 2.0 %collective-permute-start = (bf16[192,128]{1,0:T(8,128)(2,1)S(1)}, bf16[192,128]{1,0:T(8,128)(2,1)S(1)}, u32[]{:S(2)}, u32[]{:S(2)}) collective-permute-start(bf16[192,128]{1,0:T(8,128)(2,1)S(1)} %get-tuple-element.19), channel_id=1, source_target_pairs={{0,1},{1,0},{2,3},{3,2},{4,5},{5,4},{6,7},{7,6},{8,9},{9,8},{10,11... | collective-permute-start | bytes 147464 | tf_op jit(solution)/shard_map/ppermute | solution.py:19
  9.8 2.1 %collective-permute-done.refs_1_.refs_2_ = bf16[192,128]{1,0:T(8,128)(2,1)S(1)} collective-permute-done((bf16[192,128]{1,0:T(8,128)(2,1)S(1)}, bf16[192,128]{1,0:T(8,128)(2,1)S(1)}, u32[]{:S(2)}, u32[]{:S(2)}) %collective-permute-start) | collective-permute-done | bytes 49184 | tf_op jit(solution)/shard_map/ppermute | solution.py:19
  11.9 2.1 %collective-permute-start.1 = (bf16[9,56,128]{2,1,0:T(8,128)(2,1)S(1)}, bf16[9,56,128]{2,1,0:T(8,128)(2,1)S(1)}, u32[]{:S(2)}, u32[]{:S(2)}) collective-permute-start(bf16[9,56,128]{2,1,0:T(8,128)(2,1)S(1)} %get-tuple-element.21), channel_id=1, source_target_pairs={{0,2},{4,6},{2,0},{6,4},{1,3},{5,7},{3,1},{7,5},{8,10},{12,14},{10... | collective-permute-start | bytes 387080 | tf_op jit(solution)/shard_map/ppermute | solution.py:26
  13.9 2.9 %collective-permute-done.1.refs_3_ = bf16[9,56,128]{2,1,0:T(8,128)(2,1)S(1)} collective-permute-done((bf16[9,56,128]{2,1,0:T(8,128)(2,1)S(1)}, bf16[9,56,128]{2,1,0:T(8,128)(2,1)S(1)}, u32[]{:S(2)}, u32[]{:S(2)}) %collective-permute-start.1) | collective-permute-done | bytes 129056 | tf_op jit(solution)/shard_map/ppermute | solution.py:26
  16.9 0.6 %copy-done.2 = bf16[9,56,128]{2,1,0:T(8,128)(2,1)} copy-done((bf16[9,56,128]{2,1,0:T(8,128)(2,1)}, bf16[9,56,128]{2,1,0:T(8,128)(2,1)S(1)}, u32[]{:S(2)}) %copy-start.2) | copy-done | bytes 129048
  17.5 4.0 %collective-permute-start.2 = (bf16[9,56,128]{2,1,0:T(8,128)(2,1)}, bf16[9,56,128]{2,1,0:T(8,128)(2,1)}, u32[]{:S(2)}, u32[]{:S(2)}) collective-permute-start(bf16[9,56,128]{2,1,0:T(8,128)(2,1)} %get-tuple-element.22), channel_id=1, source_target_pairs={{2,4},{6,0},{4,2},{0,6},{3,5},{7,1},{5,3},{1,7},{10,12},{14,8},{12... | collective-permute-start | bytes 387080 | tf_op jit(solution)/shard_map/ppermute | solution.py:26
  21.6 4.7 %upward.1.refs_2_ = f32[3816,128]{1,0:T(8,128)S(1)} custom-call(f32[53,72,128]{2,1,0:T(8,128)S(1)} %bitcast.13, bf16[192,128]{1,0:T(8,128)(2,1)S(1)} %collective-permute-done.refs_1_.refs_2_, bf16[192,128]{1,0:T(8,128)(2,1)S(1)} %collective-permute-done.refs_1_.refs_2_, f32[3,72,128]{2,1,0:T(8,128)S(1)} %get-tuple-element.20.refs_3_.refs_5_.refs_6_), custom_call_target="tpu_custom_call" | custom-call | flops 29306880 | bytes 3907584 | tf_op jit(solution)/shard_map/upward/pallas_call | solution.py:531
  26.3 0.0 copy-start.4
  26.3 5.4 %north.1.refs_3_ = f32[3816,128]{1,0:T(8,128)S(1)} custom-call(s32[1]{0:T(128)} %bitcast.3.refs_0_, f32[53,72,128]{2,1,0:T(8,128)S(1)} %bitcast.14, f32[3816,128]{1,0:T(8,128)S(1)} %upward.1.refs_2_, bf16[9,56,128]{2,1,0:T(8,128)(2,1)S(1)} %copy-done.3, bf16[9,56,128]{2,1,0:T(8,128)(2,1)} %collective-permute-done.2.refs_4_, ...), custom_call_target="tpu_custom_call" | custom-call | flops 29306880 | bytes 3907584 | tf_op jit(solution)/shard_map/north/pallas_call | solution.py:545
  31.7 10.3 %shard_map.113 = (f32[53,3,24,128]{3,2,1,0:T(8,128)}, f32[4,3,8,128]{3,2,1,0:T(8,128)S(1)}) custom-call(s32[1]{0:T(128)} %bitcast.refs_0_, s32[3,1,24]{2,1,0:T(1,128)S(1)} %bitcast.17, f32[53,72,128]{2,1,0:T(8,128)S(1)} %bitcast.15, f32[3816,128]{1,0:T(8,128)S(1)} %north.1.refs_3_, bf16[53,3,16,128]{3,2,1,0:T(8,128)(2,1)S(1)} %collective-permute-done.5.refs_4_, ...), custom_call_target="tpu_custom_call" | custom-call | flops 29306880 | bytes 1953792 | tf_op jit(solution)/shard_map/pallas_call | solution.py:568
  42.0 6.2 %shard_map.114 = (f32[53,3,24,128]{3,2,1,0:T(8,128)}, f32[3,8,128]{2,1,0:T(8,128)S(1)}, f32[3,8,128]{2,1,0:T(8,128)S(1)}, f32[3,8,128]{2,1,0:T(8,128)S(1)}, f32[3,8,128]{2,1,0:T(8,128)S(1)}) custom-call(s32[1]{0:T(128)} %bitcast.refs_0_, s32[3,1,24]{2,1,0:T(1,128)S(1)} %bitcast.18, f32[53,72,128]{2,1,0:T(8,128)S(1)} %bitcast.16, ...), custom_call_target="tpu_custom_call", output_to_operand_aliasing={{0}: (13, {})} | custom-call | flops 29306880 | bytes 1953792 | tf_op jit(solution)/shard_map/pallas_call | solution.py:568
  48.2 0.1 collective-permute-start.7
  48.3 1.6 %collective-permute-start.8 = (f32[3,8,128]{2,1,0:T(8,128)S(1)}, f32[3,8,128]{2,1,0:T(8,128)S(1)}, u32[]{:S(2)}, u32[]{:S(2)}) collective-permute-start(f32[3,8,128]{2,1,0:T(8,128)S(1)} %get-tuple-element.34), channel_id=1, source_target_pairs={{0,16},{8,24},{16,0},{24,8},{1,17},{9,25},{17,1},{25,9},{2,18},{10... | collective-permute-start | bytes 36872 | tf_op jit(solution)/shard_map/ppermute | solution.py:19
  49.8 1.4 %collective-permute-start.9 = (f32[3,8,128]{2,1,0:T(8,128)S(1)}, f32[3,8,128]{2,1,0:T(8,128)S(1)}, u32[]{:S(2)}, u32[]{:S(2)}) collective-permute-start(f32[3,8,128]{2,1,0:T(8,128)S(1)} %get-tuple-element.35), channel_id=1, source_target_pairs={{0,24},{8,0},{16,8},{24,16},{1,25},{9,1},{17,9},{25,17},{2,26},{10... | collective-permute-start | bytes 36872 | tf_op jit(solution)/shard_map/ppermute | solution.py:19
  51.2 0.2 collective-permute-done.7.refs_1_
  51.4 0.7 %collective-permute-done.8.refs_2_ = f32[3,8,128]{2,1,0:T(8,128)S(1)} collective-permute-done((f32[3,8,128]{2,1,0:T(8,128)S(1)}, f32[3,8,128]{2,1,0:T(8,128)S(1)}, u32[]{:S(2)}, u32[]{:S(2)}) %collective-permute-start.8) | collective-permute-done | bytes 12320 | tf_op jit(solution)/shard_map/ppermute | solution.py:19
  52.0 0.6 %collective-permute-done.9.refs_3_ = f32[3,8,128]{2,1,0:T(8,128)S(1)} collective-permute-done((f32[3,8,128]{2,1,0:T(8,128)S(1)}, f32[3,8,128]{2,1,0:T(8,128)S(1)}, u32[]{:S(2)}, u32[]{:S(2)}) %collective-permute-start.9) | collective-permute-done | bytes 12320 | tf_op jit(solution)/shard_map/ppermute | solution.py:19
  52.6 1.0 %core.1 = f32[6,64,128]{2,1,0:T(8,128)} custom-call(f32[3,8,128]{2,1,0:T(8,128)S(1)} %get-tuple-element.32.refs_0_, f32[3,8,128]{2,1,0:T(8,128)S(1)} %collective-permute-done.7.refs_1_, f32[3,8,128]{2,1,0:T(8,128)S(1)} %collective-permute-done.8.refs_2_, f32[3,8,128]{2,1,0:T(8,128)S(1)} %collective-permute-done.9.refs_3_), custom_call_target="tpu_custom_call" | custom-call | tf_op jit(solution)/shard_map/core/pallas_call | solution.py:599
  (14 shorter events, 0.0 us)
Async XLA Ops:
  0.6 1.5 %copy-start = (f32[53,3,24,128]{3,2,1,0:T(8,128)S(1)}, f32[53,3,24,128]{3,2,1,0:T(8,128)}, u32[]{:S(2)}) copy-start(f32[53,3,24,128]{3,2,1,0:T(8,128)} %param.10) | copy-start | bytes 5861380
  2.2 19.4 %copy-start.1 = (f32[53,3,24,128]{3,2,1,0:T(8,128)S(1)}, f32[53,3,24,128]{3,2,1,0:T(8,128)}, u32[]{:S(2)}) copy-start(f32[53,3,24,128]{3,2,1,0:T(8,128)} %param.10) | copy-start | bytes 5861380
  4.5 27.2 %collective-permute-start.6 = (bf16[53,3,16,128]{3,2,1,0:T(8,128)(2,1)}, bf16[53,3,16,128]{3,2,1,0:T(8,128)(2,1)S(1)}, u32[]{:S(2)}, u32[]{:S(2)}) collective-permute-start(bf16[53,3,16,128]{3,2,1,0:T(8,128)(2,1)} %get-tuple-element.28), channel_id=1, source_target_pairs={{8,16},{24,0},{16,8},{0,24},{9,17},{25,1},{17,9},{1,25},{10,18},{2... | collective-permute-start | bytes 1953800 | tf_op jit(solution)/shard_map/ppermute | solution.py:26
  7.0 24.7 %collective-permute-start.5 = (bf16[53,3,16,128]{3,2,1,0:T(8,128)(2,1)}, bf16[53,3,16,128]{3,2,1,0:T(8,128)(2,1)S(1)}, u32[]{:S(2)}, u32[]{:S(2)}) collective-permute-start(bf16[53,3,16,128]{3,2,1,0:T(8,128)(2,1)} %get-tuple-element.28), channel_id=1, source_target_pairs={{0,8},{16,24},{8,0},{24,16},{1,9},{17,25},{9,1},{25,17},{2,10},{18... | collective-permute-start | bytes 1953800 | tf_op jit(solution)/shard_map/ppermute | solution.py:26
  7.6 34.4 %collective-permute-start.4 = (bf16[53,3,8,128]{3,2,1,0:T(8,128)(2,1)}, bf16[53,3,8,128]{3,2,1,0:T(8,128)(2,1)}, u32[]{:S(2)}, u32[]{:S(2)}) collective-permute-start(bf16[53,3,8,128]{3,2,1,0:T(8,128)(2,1)} %get-tuple-element.23), channel_id=1, source_target_pairs={{8,16},{24,0},{16,8},{0,24},{9,17},{25,1},{17,9},{1,25},{10,18},{2... | collective-permute-start | bytes 976904 | tf_op jit(solution)/shard_map/ppermute | solution.py:26
  7.7 34.3 %collective-permute-start.3 = (bf16[53,3,8,128]{3,2,1,0:T(8,128)(2,1)}, bf16[53,3,8,128]{3,2,1,0:T(8,128)(2,1)}, u32[]{:S(2)}, u32[]{:S(2)}) collective-permute-start(bf16[53,3,8,128]{3,2,1,0:T(8,128)(2,1)} %get-tuple-element.23), channel_id=1, source_target_pairs={{0,8},{16,24},{8,0},{24,16},{1,9},{17,25},{9,1},{25,17},{2,10},{18... | collective-permute-start | bytes 976904 | tf_op jit(solution)/shard_map/ppermute | solution.py:26
  7.8 4.1 %collective-permute-start = (bf16[192,128]{1,0:T(8,128)(2,1)S(1)}, bf16[192,128]{1,0:T(8,128)(2,1)S(1)}, u32[]{:S(2)}, u32[]{:S(2)}) collective-permute-start(bf16[192,128]{1,0:T(8,128)(2,1)S(1)} %get-tuple-element.19), channel_id=1, source_target_pairs={{0,1},{1,0},{2,3},{3,2},{4,5},{5,4},{6,7},{7,6},{8,9},{9,8},{10,11... | collective-permute-start | bytes 147464 | tf_op jit(solution)/shard_map/ppermute | solution.py:19
  11.9 5.0 %collective-permute-start.1 = (bf16[9,56,128]{2,1,0:T(8,128)(2,1)S(1)}, bf16[9,56,128]{2,1,0:T(8,128)(2,1)S(1)}, u32[]{:S(2)}, u32[]{:S(2)}) collective-permute-start(bf16[9,56,128]{2,1,0:T(8,128)(2,1)S(1)} %get-tuple-element.21), channel_id=1, source_target_pairs={{0,2},{4,6},{2,0},{6,4},{1,3},{5,7},{3,1},{7,5},{8,10},{12,14},{10... | collective-permute-start | bytes 387080 | tf_op jit(solution)/shard_map/ppermute | solution.py:26
  16.9 0.6 %copy-start.2 = (bf16[9,56,128]{2,1,0:T(8,128)(2,1)}, bf16[9,56,128]{2,1,0:T(8,128)(2,1)S(1)}, u32[]{:S(2)}) copy-start(bf16[9,56,128]{2,1,0:T(8,128)(2,1)S(1)} %collective-permute-done.1.refs_3_) | copy-start | bytes 387076
  17.5 8.8 %collective-permute-start.2 = (bf16[9,56,128]{2,1,0:T(8,128)(2,1)}, bf16[9,56,128]{2,1,0:T(8,128)(2,1)}, u32[]{:S(2)}, u32[]{:S(2)}) collective-permute-start(bf16[9,56,128]{2,1,0:T(8,128)(2,1)} %get-tuple-element.22), channel_id=1, source_target_pairs={{2,4},{6,0},{4,2},{0,6},{3,5},{7,1},{5,3},{1,7},{10,12},{14,8},{12... | collective-permute-start | bytes 387080 | tf_op jit(solution)/shard_map/ppermute | solution.py:26
  21.6 4.7 %copy-start.3 = (bf16[9,56,128]{2,1,0:T(8,128)(2,1)S(1)}, bf16[9,56,128]{2,1,0:T(8,128)(2,1)}, u32[]{:S(2)}) copy-start(bf16[9,56,128]{2,1,0:T(8,128)(2,1)} %copy-done.2) | copy-start | bytes 387076
  26.3 5.4 %copy-start.4 = (f32[3,64]{1,0:T(4,128)S(1)}, f32[3,64]{1,0:T(4,128)}, u32[]{:S(2)}) copy-start(f32[3,64]{1,0:T(4,128)} %refs_11_.3) | copy-start | bytes 2308
  26.3 5.4 %copy-start.5 = (s32[1,3,24,1]{2,3,1,0:T(1,128)S(1)}, s32[1,3,24,1]{2,3,1,0:T(1,128)}, u32[]{:S(2)}) copy-start(s32[1,3,24,1]{2,3,1,0:T(1,128)} %param.13) | copy-start | bytes 868
  48.2 3.2 %collective-permute-start.7 = (f32[3,8,128]{2,1,0:T(8,128)S(1)}, f32[3,8,128]{2,1,0:T(8,128)S(1)}, u32[]{:S(2)}, u32[]{:S(2)}) collective-permute-start(f32[3,8,128]{2,1,0:T(8,128)S(1)} %get-tuple-element.33), channel_id=1, source_target_pairs={{0,8},{8,16},{16,24},{24,0},{1,9},{9,17},{17,25},{25,1},{2,10},{10... | collective-permute-start | bytes 36872 | tf_op jit(solution)/shard_map/ppermute | solution.py:19
  48.3 3.8 %collective-permute-start.8 = (f32[3,8,128]{2,1,0:T(8,128)S(1)}, f32[3,8,128]{2,1,0:T(8,128)S(1)}, u32[]{:S(2)}, u32[]{:S(2)}) collective-permute-start(f32[3,8,128]{2,1,0:T(8,128)S(1)} %get-tuple-element.34), channel_id=1, source_target_pairs={{0,16},{8,24},{16,0},{24,8},{1,17},{9,25},{17,1},{25,9},{2,18},{10... | collective-permute-start | bytes 36872 | tf_op jit(solution)/shard_map/ppermute | solution.py:19
  49.8 2.8 %collective-permute-start.9 = (f32[3,8,128]{2,1,0:T(8,128)S(1)}, f32[3,8,128]{2,1,0:T(8,128)S(1)}, u32[]{:S(2)}, u32[]{:S(2)}) collective-permute-start(f32[3,8,128]{2,1,0:T(8,128)S(1)} %get-tuple-element.35), channel_id=1, source_target_pairs={{0,24},{8,0},{16,8},{24,16},{1,25},{9,1},{17,9},{25,17},{2,26},{10... | collective-permute-start | bytes 36872 | tf_op jit(solution)/shard_map/ppermute | solution.py:19
where the time goes:
time: 54 us; the launch traced here: 53.7 us
  Pallas kernels  29.8 us (55%)
  starting transfers between devices  14.4 us (27%)
  waiting for transfers between devices  6.42 us (12%)
  local copies, waits for them, and re-layouts  2.2 us (4%)
  between operations  0.78 us (1%)
    pallas_call x2, Pallas kernels, body(): pl.pallas_call(lambda *refs, first=first, last=last, span=span: chunk_ker...  16.5 us
    ppermute x6, starting transfers between devices, swap(): return lax.ppermute(array, axis, pairs + [(b, a) for a, b in pairs])  9.42 us
    pallas_call x1, Pallas kernels, body(): pl.pallas_call(lambda *refs: north_kernel(*refs, species=species, width_x...  5.37 us
    ppermute x4, starting transfers between devices, shift(): lax.ppermute(array, axis, [(i, (i + by) % count) for i in range(count)])  5.01 us
    pallas_call x1, Pallas kernels, body(): pl.pallas_call(lambda *refs: upward_kernel(*refs, species=species, pencil...  4.67 us
    ppermute x4, waiting for transfers between devices, shift(): lax.ppermute(array, axis, [(i, (i + by) % count) for i in range(count)])  3.48 us
    ppermute x6, waiting for transfers between devices, swap(): return lax.ppermute(array, axis, pairs + [(b, a) for a, b in pairs])  2.94 us
    pallas_call x1, Pallas kernels, body(): pl.pallas_call(lambda *refs: prep_kernel(*refs, species=species, width_x=...  2.29 us
  transfers between devices with their start and end apart: 10, of which 5 were waited for; matrix products, arithmetic and copies ran while one was open for 0% of the time, Pallas kernels for 38%

commit v1 on v0

--- a/solution.py
+++ b/solution.py
@@ -99,13 +99,24 @@
 
 
 def prep_kernel(
-    spot_ref, u_ref, *refs,
+    spot_ref, u_hbm, *refs,
     species, width_x, width_y, row_tiles, spans,
 ):
     sources, refs = refs[:7], refs[7:]
     chunk_refs, refs = refs[: len(spans)], refs[len(spans) :]
     early_ref, late_ref, zpack_ref, order_ref, net_ref, heat_ref, wind_ref, scale_ref = refs[:8]
-    zwide_ref, orders_ref, log_ref, energy_ref, net_in_ref, heat_in_ref, sems = refs[8:]
+    u_ref, zwide_ref, orders_ref, log_ref, energy_ref, net_in_ref, heat_in_ref = refs[8:15]
+    sems, u_sems = refs[15:]
+    pieces = u_sems.shape[0]
+    bounds = [species * i // pieces for i in range(pieces + 1)]
+    arrivals = [
+        pltpu.make_async_copy(
+            u_hbm.at[pl.ds(a, b - a)], u_ref.at[pl.ds(a, b - a)], u_sems.at[i]
+        )
+        for i, (a, b) in enumerate(zip(bounds, bounds[1:]))
+    ]
+    for copy in arrivals:
+        copy.start()
     targets = (wind_ref, scale_ref, orders_ref, log_ref, energy_ref, net_in_ref, heat_in_ref)
     copies = [
         pltpu.make_async_copy(source, target, sems.at[i])
@@ -114,11 +125,13 @@
     for copy in copies:
         copy.start()
     pencils = width_x * width_y
-    for c, (y0, y1) in enumerate(spans):
-        for x in range(width_x):
-            chunk_refs[c][:, x] = u_ref[
-                :, x * width_y + y0 : x * width_y + y1, :
-            ].astype(jnp.bfloat16)
+    for copy, a, b in zip(arrivals, bounds, bounds[1:]):
+        copy.wait()
+        for c, (y0, y1) in enumerate(spans):
+            for x in range(width_x):
+                chunk_refs[c][a:b, x] = u_ref[
+                    a:b, x * width_y + y0 : x * width_y + y1, :
+                ].astype(jnp.bfloat16)
     flat = u_ref.reshape(species * pencils, LANES)
     odd = lax.rem(spot_ref[0], 2)
     for g, s0 in enumerate(groups_of(species)):
@@ -243,7 +256,7 @@
 
 
 def north_kernel(
-    spot_ref, u_ref, z_ref, early_ref, late_ref, v_ref, out_ref, acc_ref,
+    spot_ref, u_ref, early_ref, late_ref, v_ref, acc_ref,
     *, species, width_x, width_y,
 ):
     pencils = width_x * width_y
@@ -279,16 +292,9 @@
 
     lax.fori_loop(0, count * width_x, north, 0)
 
-    def close_up(s, carry):
-        at = pl.ds(pl.multiple_of(s * pencils, OCTET), pencils)
-        out_ref[at, :] = flat[at, :] - (flow_step / 6.0) * (acc_ref[at, :] + z_ref[at, :])
-        return carry
-
-    lax.fori_loop(0, species, close_up, 0)
-
 
 def chunk_kernel(
-    me_ref, hot_ref, u_ref, part_ref, early_ref, late_ref, wind_ref, scale_ref,
+    me_ref, hot_ref, u_ref, part_ref, raised_ref, early_ref, late_ref, wind_ref, scale_ref,
     order_ref, net_ref, heat_ref, basis_ref, *refs,
     species, width_x, span, members, share, first, last,
 ):
@@ -309,6 +315,7 @@
     width_y = scale_ref.shape[1]
     u_ref = u_ref.reshape(species, width_x, width_y, LANES)
     part_ref = part_ref.reshape(species, width_x, width_y, LANES)
+    raised_ref = raised_ref.reshape(species, width_x, width_y, LANES)
 
     def east(s, low_ref, high_ref):
         for o in range(octets):
@@ -323,7 +330,8 @@
                 return u_ref[s, i, there]
 
             def put(i, value):
-                out_ref[s, i, at] = part_ref[s, i, there] - (flow_step / 6.0) * value
+                others = part_ref[s, i, there] + raised_ref[s, i, there]
+                out_ref[s, i, at] = u_ref[s, i, there] - (flow_step / 6.0) * (value + others)
 
             line(load, width_x, lambda i: wind_ref[0, i * width_y + there.start : i * width_y + there.stop], put)
 
@@ -382,6 +390,7 @@
             source = jnp.dot(net, rates, preferred_element_type=jnp.float32)
             current = current + sub_step * rounded(source)
         increment = rounded(current - start)
+        gains = []
         for y in range(OCTET):
             cols = slice(y * LANES, (y + 1) * LANES)
             row = y0 + o * OCTET + y
@@ -391,10 +400,16 @@
                 flat[pl.ds(s0 * rows + at, size, stride=rows), :] = (
                     cells_ref[block, s0 : s0 + size, cols] + gain[s0 : s0 + size, :]
                 )
-            sums = jnp.dot(heat, gain.astype(jnp.bfloat16), preferred_element_type=jnp.float32)
-            release_ref[row // share, x, row % share : row % share + 1, :] = (
-                sums[0:1] + sums[1:2] + sums[2:3]
-            )
+            gains.append(gain.astype(jnp.bfloat16))
+        sums = jnp.dot(
+            heat, jnp.concatenate(gains, axis=1), preferred_element_type=jnp.float32
+        )
+        sums = sums[0:1] + sums[1:2] + sums[2:3]
+        for y in range(OCTET):
+            row = y0 + o * OCTET + y
+            release_ref[row // share, x, row % share : row % share + 1, :] = sums[
+                :, y * LANES : (y + 1) * LANES
+            ]
         if o == octets - 1:
             stores.append(
                 pltpu.make_async_copy(
@@ -468,7 +483,7 @@
     spans = [(0, cut), (cut, width_y)]
     vmem = pl.BlockSpec(memory_space=pltpu.VMEM)
     smem = pl.BlockSpec(memory_space=pltpu.SMEM)
-    flat_u = close(chemical_log_concentrations.reshape(species, pencils, depth))
+    flat_source = chemical_log_concentrations.reshape(species, pencils, depth)
     params = pltpu.CompilerParams(vmem_limit_bytes=32 * 1024 * 1024)
 
     def chunk(span):
@@ -478,13 +493,13 @@
     any_spec = pl.BlockSpec(memory_space=pl.ANY)
     me = lax.axis_index("gx").astype(jnp.int32).reshape(1)
     spot = lax.axis_index("gy").astype(jnp.int32).reshape(1)
-    *chunks, y_early, y_late, z_own, order, net, heat, wind, scale = pl.pallas_call(
+    *chunks, y_early, y_late, z_own, order, net, heat, wind, scale, flat_u = pl.pallas_call(
         lambda *refs: prep_kernel(
             *refs, species=species, width_x=width_x, width_y=width_y, row_tiles=row_tiles,
             spans=spans,
         ),
-        in_specs=[smem, vmem] + [any_spec] * 7,
-        out_specs=[vmem] * (len(spans) + 8),
+        in_specs=[smem] + [any_spec] * 8,
+        out_specs=[vmem] * (len(spans) + 9),
         out_shape=[chunk(span) for span in spans]
         + [
             side,
@@ -495,6 +510,7 @@
             jax.ShapeDtypeStruct((OCTET, padded + OCTET), jnp.bfloat16),
             pltpu.VMEM((3, pencils, depth), jnp.float32),
             pltpu.VMEM((width_x, width_y, depth), jnp.float32),
+            pltpu.VMEM((species, pencils, depth), jnp.float32),
         ],
         scratch_shapes=[
             pltpu.VMEM((OCTET * slots, LANES), jnp.float32),
@@ -504,12 +520,13 @@
             pltpu.VMEM((species, reactions), jnp.bfloat16),
             pltpu.VMEM((1, species), jnp.float32),
             pltpu.SemaphoreType.DMA((7,)),
+            pltpu.SemaphoreType.DMA((4,)),
         ],
         compiler_params=params,
         name="prep",
     )(
         spot,
-        flat_u,
+        far(flat_source),
         far(advection_wind.reshape(3, pencils, depth)),
         far(inverse_thermal_scale),
         far(kinetic_exponents.T),
@@ -544,16 +561,15 @@
     )(flat_u, close(z_low), close(z_high), wind)
     part = pl.pallas_call(
         lambda *refs: north_kernel(*refs, species=species, width_x=width_x, width_y=width_y),
-        in_specs=[smem] + [vmem] * 5,
+        in_specs=[smem] + [vmem] * 4,
         out_specs=vmem,
         out_shape=pltpu.VMEM((rows, depth), jnp.float32),
-        scratch_shapes=[pltpu.VMEM((rows, LANES), jnp.float32)],
         cost_estimate=pl.CostEstimate(
             flops=cells * 60, bytes_accessed=cells * 8, transcendentals=cells * 2
         ),
         compiler_params=params,
         name="north",
-    )(spot, flat_u, raised, close(early_rows), close(late_rows), wind)
+    )(spot, flat_u, close(early_rows), close(late_rows), wind)
     state = None
 
     hot = jnp.swapaxes(kinetics_column_switch, 2, 3).reshape(width_x, 1, width_y)
@@ -570,7 +586,7 @@
                 *refs, species=species, width_x=width_x, span=span, members=members,
                 share=share, first=first, last=last,
             ),
-            in_specs=[smem, smem] + [vmem] * 10 + ([] if first else [vmem, any_spec]),
+            in_specs=[smem, smem] + [vmem] * 11 + ([] if first else [vmem, any_spec]),
             out_specs=[any_spec] + [vmem] * len(outs),
             out_shape=[jax.ShapeDtypeStruct(chemical_log_concentrations.shape, jnp.float32)] + outs,
             scratch_shapes=([pltpu.VMEM(pile.shape, jnp.float32)] if last else [])
@@ -581,13 +597,13 @@
                 ),
                 pltpu.SemaphoreType.DMA((width_x,)),
             ],
-            input_output_aliases={} if first else {13: 0},
-            compiler_params=params,
+            input_output_aliases={} if first else {14: 0},
+            compiler_params=pltpu.CompilerParams(vmem_limit_bytes=32 * 1024 * 1024),
             cost_estimate=pl.CostEstimate(
                 flops=cells * 60, bytes_accessed=cells * 4, transcendentals=cells * 4
             ),
         )(
-            me, hot, flat_u, part, close(x_early[c]), close(x_late[c]), wind, scale, order, net, heat, streamwise_tucker_basis,
+            me, hot, flat_u, part, raised, close(x_early[c]), close(x_late[c]), wind, scale, order, net, heat, streamwise_tucker_basis,
             *([] if first else [release, state]),
         )
         state = results[0]

time: 54 us -> 53.1 us (0.983)
  local copies, waits for them, and re-layouts: 2.2 us -> 0.67 us
  Pallas kernels: 29.8 us -> 30.5 us
    unnamed x12 -> x8, local copies, waits for them, and re-layouts: 2.2 us -> 0.67 us
    pallas_call x1, Pallas kernels: 2.29 us -> 3.47 us  [body(): pl.pallas_call(lambda *refs: prep_kernel(*refs, species=species, width_x=...]
    pallas_call x1, Pallas kernels: 5.37 us -> 4.81 us  [body(): pl.pallas_call(lambda *refs: north_kernel(*refs, species=species, width_x...]
  transfers between devices with their start and end apart: 10 -> 10, of which waited for: 5 -> 5; matrix products, arithmetic and copies ran while one was open for 0% -> 0% of each run, Pallas kernels for 38% -> 37%
where the time goes in v1:
time: 53.1 us; the launch traced here: 52.8 us
  Pallas kernels  30.5 us (57%)
  starting transfers between devices  14.4 us (27%)
  waiting for transfers between devices  6.42 us (12%)
  between operations  0.77 us (1%)
  local copies, waits for them, and re-layouts  0.67 us (1%)
    pallas_call x2, Pallas kernels, body(): pl.pallas_call(lambda *refs, first=first, last=last, span=span: chunk_ker...  16.5 us
    ppermute x6, starting transfers between devices, swap(): return lax.ppermute(array, axis, pairs + [(b, a) for a, b in pairs])  9.42 us
    ppermute x4, starting transfers between devices, shift(): lax.ppermute(array, axis, [(i, (i + by) % count) for i in range(count)])  5.02 us
    pallas_call x1, Pallas kernels, body(): pl.pallas_call(lambda *refs: north_kernel(*refs, species=species, width_x...  4.81 us
    pallas_call x1, Pallas kernels, body(): pl.pallas_call(lambda *refs: upward_kernel(*refs, species=species, pencil...  4.67 us
    ppermute x4, waiting for transfers between devices, shift(): lax.ppermute(array, axis, [(i, (i + by) % count) for i in range(count)])  3.48 us
    pallas_call x1, Pallas kernels, body(): pl.pallas_call(lambda *refs: prep_kernel(*refs, species=species, width_x=...  3.47 us
    ppermute x6, waiting for transfers between devices, swap(): return lax.ppermute(array, axis, pairs + [(b, a) for a, b in pairs])  2.94 us
  transfers between devices with their start and end apart: 10, of which 5 were waited for; matrix products, arithmetic and copies ran while one was open for 0% of the time, Pallas kernels for 37%

profile of v1, /device:TPU:0, one launch (start us, length us, event | category | flops | bytes accessed | tf_op | source)
XLA Modules:
  0.0 52.8 jit_solution(8615938551533166773)
XLA Ops:
  0.6 3.5 %prep.1 = (bf16[53,3,16,128]{3,2,1,0:T(8,128)(2,1)}, bf16[53,3,8,128]{3,2,1,0:T(8,128)(2,1)}, bf16[9,56,128]{2,1,0:T(8,128)(2,1)S(1)}, bf16[9,56,128]{2,1,0:T(8,...) custom-call(s32[1]{0:T(128)} %bitcast.2.refs_0_, ...), custom_call_target="tpu_custom_call" | custom-call | tf_op jit(solution)/shard_map/prep/pallas_call | solution.py:496
  4.1 2.5 %collective-permute-start.6 = (bf16[53,3,16,128]{3,2,1,0:T(8,128)(2,1)}, bf16[53,3,16,128]{3,2,1,0:T(8,128)(2,1)S(1)}, u32[]{:S(2)}, u32[]{:S(2)}) collective-permute-start(bf16[53,3,16,128]{3,2,1,0:T(8,128)(2,1)} %get-tuple-element.30), channel_id=1, source_target_pairs={{8,16},{24,0},{16,8},{0,24},{9,17},{25,1},{17,9},{1,25},{10,18},{2... | collective-permute-start | bytes 1953800 | tf_op jit(solution)/shard_map/ppermute | solution.py:26
  6.6 0.7 %collective-permute-start.5 = (bf16[53,3,16,128]{3,2,1,0:T(8,128)(2,1)}, bf16[53,3,16,128]{3,2,1,0:T(8,128)(2,1)S(1)}, u32[]{:S(2)}, u32[]{:S(2)}) collective-permute-start(bf16[53,3,16,128]{3,2,1,0:T(8,128)(2,1)} %get-tuple-element.30), channel_id=1, source_target_pairs={{0,8},{16,24},{8,0},{24,16},{1,9},{17,25},{9,1},{25,17},{2,10},{18... | collective-permute-start | bytes 1953800 | tf_op jit(solution)/shard_map/ppermute | solution.py:26
  7.3 0.1 collective-permute-start.4
  7.3 0.1 collective-permute-start.3
  7.4 2.0 %collective-permute-start.2 = (bf16[192,128]{1,0:T(8,128)(2,1)S(1)}, bf16[192,128]{1,0:T(8,128)(2,1)S(1)}, u32[]{:S(2)}, u32[]{:S(2)}) collective-permute-start(bf16[192,128]{1,0:T(8,128)(2,1)S(1)} %get-tuple-element.24), channel_id=1, source_target_pairs={{0,1},{1,0},{2,3},{3,2},{4,5},{5,4},{6,7},{7,6},{8,9},{9,8},{10,11... | collective-permute-start | bytes 147464 | tf_op jit(solution)/shard_map/ppermute | solution.py:19
  9.4 2.1 %collective-permute-done.2.refs_1_.refs_2_ = bf16[192,128]{1,0:T(8,128)(2,1)S(1)} collective-permute-done((bf16[192,128]{1,0:T(8,128)(2,1)S(1)}, bf16[192,128]{1,0:T(8,128)(2,1)S(1)}, u32[]{:S(2)}, u32[]{:S(2)}) %collective-permute-start.2) | collective-permute-done | bytes 49184 | tf_op jit(solution)/shard_map/ppermute | solution.py:19
  11.5 2.1 %collective-permute-start = (bf16[9,56,128]{2,1,0:T(8,128)(2,1)S(1)}, bf16[9,56,128]{2,1,0:T(8,128)(2,1)S(1)}, u32[]{:S(2)}, u32[]{:S(2)}) collective-permute-start(bf16[9,56,128]{2,1,0:T(8,128)(2,1)S(1)} %get-tuple-element.21), channel_id=1, source_target_pairs={{0,2},{4,6},{2,0},{6,4},{1,3},{5,7},{3,1},{7,5},{8,10},{12,14},{10... | collective-permute-start | bytes 387080 | tf_op jit(solution)/shard_map/ppermute | solution.py:26
  13.6 2.9 %collective-permute-done.refs_2_ = bf16[9,56,128]{2,1,0:T(8,128)(2,1)S(1)} collective-permute-done((bf16[9,56,128]{2,1,0:T(8,128)(2,1)S(1)}, bf16[9,56,128]{2,1,0:T(8,128)(2,1)S(1)}, u32[]{:S(2)}, u32[]{:S(2)}) %collective-permute-start) | collective-permute-done | bytes 129056 | tf_op jit(solution)/shard_map/ppermute | solution.py:26
  16.5 0.7 %copy-done = bf16[9,56,128]{2,1,0:T(8,128)(2,1)} copy-done((bf16[9,56,128]{2,1,0:T(8,128)(2,1)}, bf16[9,56,128]{2,1,0:T(8,128)(2,1)S(1)}, u32[]{:S(2)}) %copy-start) | copy-done | bytes 129048
  17.2 4.0 %collective-permute-start.1 = (bf16[9,56,128]{2,1,0:T(8,128)(2,1)}, bf16[9,56,128]{2,1,0:T(8,128)(2,1)}, u32[]{:S(2)}, u32[]{:S(2)}) collective-permute-start(bf16[9,56,128]{2,1,0:T(8,128)(2,1)} %get-tuple-element.22), channel_id=1, source_target_pairs={{2,4},{6,0},{4,2},{0,6},{3,5},{7,1},{5,3},{1,7},{10,12},{14,8},{12... | collective-permute-start | bytes 387080 | tf_op jit(solution)/shard_map/ppermute | solution.py:26
  21.2 4.7 %upward.1.refs_4_ = f32[3816,128]{1,0:T(8,128)S(1)} custom-call(f32[53,72,128]{2,1,0:T(8,128)S(1)} %get-tuple-element.20.refs_1_.refs_0_.refs_2_, bf16[192,128]{1,0:T(8,128)(2,1)S(1)} %collective-permute-done.2.refs_1_.refs_2_, bf16[192,128]{1,0:T(8,128)(2,1)S(1)} %collective-permute-done.2.refs_1_.refs_2_, ...), custom_call_target="tpu_custom_call" | custom-call | flops 29306880 | bytes 3907584 | tf_op jit(solution)/shard_map/upward/pallas_call | solution.py:548
  25.9 0.0 copy-start.2
  25.9 0.0 copy-start.3
  25.9 4.8 %north.1.refs_3_ = f32[3816,128]{1,0:T(8,128)S(1)} custom-call(s32[1]{0:T(128)} %bitcast.2.refs_0_, f32[53,72,128]{2,1,0:T(8,128)S(1)} %get-tuple-element.20.refs_1_.refs_0_.refs_2_, bf16[9,56,128]{2,1,0:T(8,128)(2,1)S(1)} %copy-done.1, bf16[9,56,128]{2,1,0:T(8,128)(2,1)} %collective-permute-done.1.refs_3_, ...), custom_call_target="tpu_custom_call" | custom-call | flops 29306880 | bytes 3907584 | tf_op jit(solution)/shard_map/north/pallas_call | solution.py:562
  30.8 10.3 %shard_map.113 = (f32[53,3,24,128]{3,2,1,0:T(8,128)}, f32[4,3,8,128]{3,2,1,0:T(8,128)S(1)}) custom-call(s32[1]{0:T(128)} %bitcast.refs_0_, s32[3,1,24]{2,1,0:T(1,128)S(1)} %bitcast.12, f32[53,72,128]{2,1,0:T(8,128)S(1)} %get-tuple-element.20.refs_1_.refs_0_.refs_2_, f32[3816,128]{1,0:T(8,128)S(1)} %north.1.refs_3_, f32[3816,128]{1,0:T(8,128)S(1)} %upward.1.refs_4_, ...), custom_call_target="tpu_custom_call" | custom-call | flops 29306880 | bytes 1953792 | tf_op jit(solution)/shard_map/pallas_call | solution.py:584
  41.1 6.2 %shard_map.114 = (f32[53,3,24,128]{3,2,1,0:T(8,128)}, f32[3,8,128]{2,1,0:T(8,128)S(1)}, f32[3,8,128]{2,1,0:T(8,128)S(1)}, f32[3,8,128]{2,1,0:T(8,128)S(1)}, f32[3,8,128]{2,1,0:T(8,128)S(1)}) custom-call(s32[1]{0:T(128)} %bitcast.refs_0_, s32[3,1,24]{2,1,0:T(1,128)S(1)} %bitcast.13, ...), custom_call_target="tpu_custom_call", output_to_operand_aliasing={{0}: (14, {})} | custom-call | flops 29306880 | bytes 1953792 | tf_op jit(solution)/shard_map/pallas_call | solution.py:584
  47.3 0.1 collective-permute-start.7
  47.4 1.6 %collective-permute-start.8 = (f32[3,8,128]{2,1,0:T(8,128)S(1)}, f32[3,8,128]{2,1,0:T(8,128)S(1)}, u32[]{:S(2)}, u32[]{:S(2)}) collective-permute-start(f32[3,8,128]{2,1,0:T(8,128)S(1)} %get-tuple-element.36), channel_id=1, source_target_pairs={{0,16},{8,24},{16,0},{24,8},{1,17},{9,25},{17,1},{25,9},{2,18},{10... | collective-permute-start | bytes 36872 | tf_op jit(solution)/shard_map/ppermute | solution.py:19
  48.9 1.4 %collective-permute-start.9 = (f32[3,8,128]{2,1,0:T(8,128)S(1)}, f32[3,8,128]{2,1,0:T(8,128)S(1)}, u32[]{:S(2)}, u32[]{:S(2)}) collective-permute-start(f32[3,8,128]{2,1,0:T(8,128)S(1)} %get-tuple-element.37), channel_id=1, source_target_pairs={{0,24},{8,0},{16,8},{24,16},{1,25},{9,1},{17,9},{25,17},{2,26},{10... | collective-permute-start | bytes 36872 | tf_op jit(solution)/shard_map/ppermute | solution.py:19
  50.3 0.2 collective-permute-done.7.refs_1_
  50.5 0.7 %collective-permute-done.8.refs_2_ = f32[3,8,128]{2,1,0:T(8,128)S(1)} collective-permute-done((f32[3,8,128]{2,1,0:T(8,128)S(1)}, f32[3,8,128]{2,1,0:T(8,128)S(1)}, u32[]{:S(2)}, u32[]{:S(2)}) %collective-permute-start.8) | collective-permute-done | bytes 12320 | tf_op jit(solution)/shard_map/ppermute | solution.py:19
  51.1 0.6 %collective-permute-done.9.refs_3_ = f32[3,8,128]{2,1,0:T(8,128)S(1)} collective-permute-done((f32[3,8,128]{2,1,0:T(8,128)S(1)}, f32[3,8,128]{2,1,0:T(8,128)S(1)}, u32[]{:S(2)}, u32[]{:S(2)}) %collective-permute-start.9) | collective-permute-done | bytes 12320 | tf_op jit(solution)/shard_map/ppermute | solution.py:19
  51.7 1.0 %core.1 = f32[6,64,128]{2,1,0:T(8,128)} custom-call(f32[3,8,128]{2,1,0:T(8,128)S(1)} %get-tuple-element.34.refs_0_, f32[3,8,128]{2,1,0:T(8,128)S(1)} %collective-permute-done.7.refs_1_, f32[3,8,128]{2,1,0:T(8,128)S(1)} %collective-permute-done.8.refs_2_, f32[3,8,128]{2,1,0:T(8,128)S(1)} %collective-permute-done.9.refs_3_), custom_call_target="tpu_custom_call" | custom-call | tf_op jit(solution)/shard_map/core/pallas_call | solution.py:615
  (10 shorter events, 0.0 us)
Async XLA Ops:
  4.1 26.6 %collective-permute-start.6 = (bf16[53,3,16,128]{3,2,1,0:T(8,128)(2,1)}, bf16[53,3,16,128]{3,2,1,0:T(8,128)(2,1)S(1)}, u32[]{:S(2)}, u32[]{:S(2)}) collective-permute-start(bf16[53,3,16,128]{3,2,1,0:T(8,128)(2,1)} %get-tuple-element.30), channel_id=1, source_target_pairs={{8,16},{24,0},{16,8},{0,24},{9,17},{25,1},{17,9},{1,25},{10,18},{2... | collective-permute-start | bytes 1953800 | tf_op jit(solution)/shard_map/ppermute | solution.py:26
  6.6 24.2 %collective-permute-start.5 = (bf16[53,3,16,128]{3,2,1,0:T(8,128)(2,1)}, bf16[53,3,16,128]{3,2,1,0:T(8,128)(2,1)S(1)}, u32[]{:S(2)}, u32[]{:S(2)}) collective-permute-start(bf16[53,3,16,128]{3,2,1,0:T(8,128)(2,1)} %get-tuple-element.30), channel_id=1, source_target_pairs={{0,8},{16,24},{8,0},{24,16},{1,9},{17,25},{9,1},{25,17},{2,10},{18... | collective-permute-start | bytes 1953800 | tf_op jit(solution)/shard_map/ppermute | solution.py:26
  7.3 33.8 %collective-permute-start.4 = (bf16[53,3,8,128]{3,2,1,0:T(8,128)(2,1)}, bf16[53,3,8,128]{3,2,1,0:T(8,128)(2,1)}, u32[]{:S(2)}, u32[]{:S(2)}) collective-permute-start(bf16[53,3,8,128]{3,2,1,0:T(8,128)(2,1)} %get-tuple-element.25), channel_id=1, source_target_pairs={{8,16},{24,0},{16,8},{0,24},{9,17},{25,1},{17,9},{1,25},{10,18},{2... | collective-permute-start | bytes 976904 | tf_op jit(solution)/shard_map/ppermute | solution.py:26
  7.3 33.8 %collective-permute-start.3 = (bf16[53,3,8,128]{3,2,1,0:T(8,128)(2,1)}, bf16[53,3,8,128]{3,2,1,0:T(8,128)(2,1)}, u32[]{:S(2)}, u32[]{:S(2)}) collective-permute-start(bf16[53,3,8,128]{3,2,1,0:T(8,128)(2,1)} %get-tuple-element.25), channel_id=1, source_target_pairs={{0,8},{16,24},{8,0},{24,16},{1,9},{17,25},{9,1},{25,17},{2,10},{18... | collective-permute-start | bytes 976904 | tf_op jit(solution)/shard_map/ppermute | solution.py:26
  7.4 4.1 %collective-permute-start.2 = (bf16[192,128]{1,0:T(8,128)(2,1)S(1)}, bf16[192,128]{1,0:T(8,128)(2,1)S(1)}, u32[]{:S(2)}, u32[]{:S(2)}) collective-permute-start(bf16[192,128]{1,0:T(8,128)(2,1)S(1)} %get-tuple-element.24), channel_id=1, source_target_pairs={{0,1},{1,0},{2,3},{3,2},{4,5},{5,4},{6,7},{7,6},{8,9},{9,8},{10,11... | collective-permute-start | bytes 147464 | tf_op jit(solution)/shard_map/ppermute | solution.py:19
  11.5 5.0 %collective-permute-start = (bf16[9,56,128]{2,1,0:T(8,128)(2,1)S(1)}, bf16[9,56,128]{2,1,0:T(8,128)(2,1)S(1)}, u32[]{:S(2)}, u32[]{:S(2)}) collective-permute-start(bf16[9,56,128]{2,1,0:T(8,128)(2,1)S(1)} %get-tuple-element.21), channel_id=1, source_target_pairs={{0,2},{4,6},{2,0},{6,4},{1,3},{5,7},{3,1},{7,5},{8,10},{12,14},{10... | collective-permute-start | bytes 387080 | tf_op jit(solution)/shard_map/ppermute | solution.py:26
  16.5 0.7 %copy-start = (bf16[9,56,128]{2,1,0:T(8,128)(2,1)}, bf16[9,56,128]{2,1,0:T(8,128)(2,1)S(1)}, u32[]{:S(2)}) copy-start(bf16[9,56,128]{2,1,0:T(8,128)(2,1)S(1)} %collective-permute-done.refs_2_) | copy-start | bytes 387076
  17.2 8.8 %collective-permute-start.1 = (bf16[9,56,128]{2,1,0:T(8,128)(2,1)}, bf16[9,56,128]{2,1,0:T(8,128)(2,1)}, u32[]{:S(2)}, u32[]{:S(2)}) collective-permute-start(bf16[9,56,128]{2,1,0:T(8,128)(2,1)} %get-tuple-element.22), channel_id=1, source_target_pairs={{2,4},{6,0},{4,2},{0,6},{3,5},{7,1},{5,3},{1,7},{10,12},{14,8},{12... | collective-permute-start | bytes 387080 | tf_op jit(solution)/shard_map/ppermute | solution.py:26
  21.2 4.7 %copy-start.1 = (bf16[9,56,128]{2,1,0:T(8,128)(2,1)S(1)}, bf16[9,56,128]{2,1,0:T(8,128)(2,1)}, u32[]{:S(2)}) copy-start(bf16[9,56,128]{2,1,0:T(8,128)(2,1)} %copy-done) | copy-start | bytes 387076
  25.9 4.9 %copy-start.2 = (f32[3,64]{1,0:T(4,128)S(1)}, f32[3,64]{1,0:T(4,128)}, u32[]{:S(2)}) copy-start(f32[3,64]{1,0:T(4,128)} %refs_12_.3) | copy-start | bytes 2308
  25.9 4.9 %copy-start.3 = (s32[1,3,24,1]{2,3,1,0:T(1,128)S(1)}, s32[1,3,24,1]{2,3,1,0:T(1,128)}, u32[]{:S(2)}) copy-start(s32[1,3,24,1]{2,3,1,0:T(1,128)} %param.13) | copy-start | bytes 868
  47.3 3.2 %collective-permute-start.7 = (f32[3,8,128]{2,1,0:T(8,128)S(1)}, f32[3,8,128]{2,1,0:T(8,128)S(1)}, u32[]{:S(2)}, u32[]{:S(2)}) collective-permute-start(f32[3,8,128]{2,1,0:T(8,128)S(1)} %get-tuple-element.35), channel_id=1, source_target_pairs={{0,8},{8,16},{16,24},{24,0},{1,9},{9,17},{17,25},{25,1},{2,10},{10... | collective-permute-start | bytes 36872 | tf_op jit(solution)/shard_map/ppermute | solution.py:19
  47.4 3.8 %collective-permute-start.8 = (f32[3,8,128]{2,1,0:T(8,128)S(1)}, f32[3,8,128]{2,1,0:T(8,128)S(1)}, u32[]{:S(2)}, u32[]{:S(2)}) collective-permute-start(f32[3,8,128]{2,1,0:T(8,128)S(1)} %get-tuple-element.36), channel_id=1, source_target_pairs={{0,16},{8,24},{16,0},{24,8},{1,17},{9,25},{17,1},{25,9},{2,18},{10... | collective-permute-start | bytes 36872 | tf_op jit(solution)/shard_map/ppermute | solution.py:19
  48.9 2.8 %collective-permute-start.9 = (f32[3,8,128]{2,1,0:T(8,128)S(1)}, f32[3,8,128]{2,1,0:T(8,128)S(1)}, u32[]{:S(2)}, u32[]{:S(2)}) collective-permute-start(f32[3,8,128]{2,1,0:T(8,128)S(1)} %get-tuple-element.37), channel_id=1, source_target_pairs={{0,24},{8,0},{16,8},{24,16},{1,25},{9,1},{17,9},{25,17},{2,26},{10... | collective-permute-start | bytes 36872 | tf_op jit(solution)/shard_map/ppermute | solution.py:19

commit v2 on v1

--- a/solution.py
+++ b/solution.py
@@ -379,16 +379,20 @@
                 sublane < 3, theta, jnp.where(sublane < 6, 1.0, 0.0)
             )
     stores = []
-    for block in range(width_x * octets):
-        x, o = block // octets, block % octets
-        start = rounded(cells_ref[block])
-        current = start
-        for _ in range(SUBSTEPS):
-            features = current.astype(jnp.bfloat16)
-            exponent = jnp.dot(order, features, preferred_element_type=jnp.float32)
+    blocks = range(width_x * octets)
+    begun = [rounded(cells_ref[block]) for block in blocks]
+    reached = list(begun)
+    for _ in range(SUBSTEPS):
+        for block in blocks:
+            exponent = jnp.dot(
+                order, reached[block].astype(jnp.bfloat16), preferred_element_type=jnp.float32
+            )
             rates = jnp.exp(exponent).astype(jnp.bfloat16)
             source = jnp.dot(net, rates, preferred_element_type=jnp.float32)
-            current = current + sub_step * rounded(source)
+            reached[block] = reached[block] + sub_step * rounded(source)
+    for block in blocks:
+        x, o = block // octets, block % octets
+        start, current = begun[block], reached[block]
         increment = rounded(current - start)
         gains = []
         for y in range(OCTET):

time: 53.1 us -> 51.3 us (0.966)
  Pallas kernels: 30.5 us -> 28.7 us
    pallas_call x2, Pallas kernels: 16.5 us -> 14.7 us  [body(): pl.pallas_call(lambda *refs, first=first, last=last, span=span: chunk_ker...]
  transfers between devices with their start and end apart: 10 -> 10, of which waited for: 5 -> 5; matrix products, arithmetic and copies ran while one was open for 0% -> 0% of each run, Pallas kernels for 37% -> 36%
where the time goes in v2:
time: 51.3 us; the launch traced here: 51 us
  Pallas kernels  28.7 us (56%)
  starting transfers between devices  14.4 us (28%)
  waiting for transfers between devices  6.42 us (13%)
  between operations  0.77 us (2%)
  local copies, waits for them, and re-layouts  0.67 us (1%)
    pallas_call x2, Pallas kernels, body(): pl.pallas_call(lambda *refs, first=first, last=last, span=span: chunk_ker...  14.7 us
    ppermute x6, starting transfers between devices, swap(): return lax.ppermute(array, axis, pairs + [(b, a) for a, b in pairs])  9.42 us
    ppermute x4, starting transfers between devices, shift(): lax.ppermute(array, axis, [(i, (i + by) % count) for i in range(count)])  5.01 us
    pallas_call x1, Pallas kernels, body(): pl.pallas_call(lambda *refs: north_kernel(*refs, species=species, width_x...  4.81 us
    pallas_call x1, Pallas kernels, body(): pl.pallas_call(lambda *refs: upward_kernel(*refs, species=species, pencil...  4.67 us
    ppermute x4, waiting for transfers between devices, shift(): lax.ppermute(array, axis, [(i, (i + by) % count) for i in range(count)])  3.48 us
    pallas_call x1, Pallas kernels, body(): pl.pallas_call(lambda *refs: prep_kernel(*refs, species=species, width_x=...  3.47 us
    ppermute x6, waiting for transfers between devices, swap(): return lax.ppermute(array, axis, pairs + [(b, a) for a, b in pairs])  2.94 us
  transfers between devices with their start and end apart: 10, of which 5 were waited for; matrix products, arithmetic and copies ran while one was open for 0% of the time, Pallas kernels for 36%

profile of v2, /device:TPU:0, one launch (start us, length us, event | category | flops | bytes accessed | tf_op | source)
XLA Modules:
  0.0 51.0 jit_solution(3877953310419627917)
XLA Ops:
  0.6 3.5 %prep.1 = (bf16[53,3,16,128]{3,2,1,0:T(8,128)(2,1)}, bf16[53,3,8,128]{3,2,1,0:T(8,128)(2,1)}, bf16[9,56,128]{2,1,0:T(8,128)(2,1)S(1)}, bf16[9,56,128]{2,1,0:T(8,...) custom-call(s32[1]{0:T(128)} %bitcast.2.refs_0_, ...), custom_call_target="tpu_custom_call" | custom-call | tf_op jit(solution)/shard_map/prep/pallas_call | solution.py:500
  4.1 2.5 %collective-permute-start.6 = (bf16[53,3,16,128]{3,2,1,0:T(8,128)(2,1)}, bf16[53,3,16,128]{3,2,1,0:T(8,128)(2,1)S(1)}, u32[]{:S(2)}, u32[]{:S(2)}) collective-permute-start(bf16[53,3,16,128]{3,2,1,0:T(8,128)(2,1)} %get-tuple-element.30), channel_id=1, source_target_pairs={{8,16},{24,0},{16,8},{0,24},{9,17},{25,1},{17,9},{1,25},{10,18},{2... | collective-permute-start | bytes 1953800 | tf_op jit(solution)/shard_map/ppermute | solution.py:26
  6.6 0.7 %collective-permute-start.5 = (bf16[53,3,16,128]{3,2,1,0:T(8,128)(2,1)}, bf16[53,3,16,128]{3,2,1,0:T(8,128)(2,1)S(1)}, u32[]{:S(2)}, u32[]{:S(2)}) collective-permute-start(bf16[53,3,16,128]{3,2,1,0:T(8,128)(2,1)} %get-tuple-element.30), channel_id=1, source_target_pairs={{0,8},{16,24},{8,0},{24,16},{1,9},{17,25},{9,1},{25,17},{2,10},{18... | collective-permute-start | bytes 1953800 | tf_op jit(solution)/shard_map/ppermute | solution.py:26
  7.3 0.1 collective-permute-start.4
  7.3 0.1 collective-permute-start.3
  7.4 2.0 %collective-permute-start.2 = (bf16[192,128]{1,0:T(8,128)(2,1)S(1)}, bf16[192,128]{1,0:T(8,128)(2,1)S(1)}, u32[]{:S(2)}, u32[]{:S(2)}) collective-permute-start(bf16[192,128]{1,0:T(8,128)(2,1)S(1)} %get-tuple-element.24), channel_id=1, source_target_pairs={{0,1},{1,0},{2,3},{3,2},{4,5},{5,4},{6,7},{7,6},{8,9},{9,8},{10,11... | collective-permute-start | bytes 147464 | tf_op jit(solution)/shard_map/ppermute | solution.py:19
  9.4 2.1 %collective-permute-done.2.refs_1_.refs_2_ = bf16[192,128]{1,0:T(8,128)(2,1)S(1)} collective-permute-done((bf16[192,128]{1,0:T(8,128)(2,1)S(1)}, bf16[192,128]{1,0:T(8,128)(2,1)S(1)}, u32[]{:S(2)}, u32[]{:S(2)}) %collective-permute-start.2) | collective-permute-done | bytes 49184 | tf_op jit(solution)/shard_map/ppermute | solution.py:19
  11.5 2.1 %collective-permute-start = (bf16[9,56,128]{2,1,0:T(8,128)(2,1)S(1)}, bf16[9,56,128]{2,1,0:T(8,128)(2,1)S(1)}, u32[]{:S(2)}, u32[]{:S(2)}) collective-permute-start(bf16[9,56,128]{2,1,0:T(8,128)(2,1)S(1)} %get-tuple-element.21), channel_id=1, source_target_pairs={{0,2},{4,6},{2,0},{6,4},{1,3},{5,7},{3,1},{7,5},{8,10},{12,14},{10... | collective-permute-start | bytes 387080 | tf_op jit(solution)/shard_map/ppermute | solution.py:26
  13.6 2.9 %collective-permute-done.refs_2_ = bf16[9,56,128]{2,1,0:T(8,128)(2,1)S(1)} collective-permute-done((bf16[9,56,128]{2,1,0:T(8,128)(2,1)S(1)}, bf16[9,56,128]{2,1,0:T(8,128)(2,1)S(1)}, u32[]{:S(2)}, u32[]{:S(2)}) %collective-permute-start) | collective-permute-done | bytes 129056 | tf_op jit(solution)/shard_map/ppermute | solution.py:26
  16.5 0.7 %copy-done = bf16[9,56,128]{2,1,0:T(8,128)(2,1)} copy-done((bf16[9,56,128]{2,1,0:T(8,128)(2,1)}, bf16[9,56,128]{2,1,0:T(8,128)(2,1)S(1)}, u32[]{:S(2)}) %copy-start) | copy-done | bytes 129048
  17.2 4.0 %collective-permute-start.1 = (bf16[9,56,128]{2,1,0:T(8,128)(2,1)}, bf16[9,56,128]{2,1,0:T(8,128)(2,1)}, u32[]{:S(2)}, u32[]{:S(2)}) collective-permute-start(bf16[9,56,128]{2,1,0:T(8,128)(2,1)} %get-tuple-element.22), channel_id=1, source_target_pairs={{2,4},{6,0},{4,2},{0,6},{3,5},{7,1},{5,3},{1,7},{10,12},{14,8},{12... | collective-permute-start | bytes 387080 | tf_op jit(solution)/shard_map/ppermute | solution.py:26
  21.2 4.7 %upward.1.refs_4_ = f32[3816,128]{1,0:T(8,128)S(1)} custom-call(f32[53,72,128]{2,1,0:T(8,128)S(1)} %get-tuple-element.20.refs_1_.refs_0_.refs_2_, bf16[192,128]{1,0:T(8,128)(2,1)S(1)} %collective-permute-done.2.refs_1_.refs_2_, bf16[192,128]{1,0:T(8,128)(2,1)S(1)} %collective-permute-done.2.refs_1_.refs_2_, ...), custom_call_target="tpu_custom_call" | custom-call | flops 29306880 | bytes 3907584 | tf_op jit(solution)/shard_map/upward/pallas_call | solution.py:552
  25.9 0.0 copy-start.2
  25.9 0.0 copy-start.3
  25.9 4.8 %north.1.refs_3_ = f32[3816,128]{1,0:T(8,128)S(1)} custom-call(s32[1]{0:T(128)} %bitcast.2.refs_0_, f32[53,72,128]{2,1,0:T(8,128)S(1)} %get-tuple-element.20.refs_1_.refs_0_.refs_2_, bf16[9,56,128]{2,1,0:T(8,128)(2,1)S(1)} %copy-done.1, bf16[9,56,128]{2,1,0:T(8,128)(2,1)} %collective-permute-done.1.refs_3_, ...), custom_call_target="tpu_custom_call" | custom-call | flops 29306880 | bytes 3907584 | tf_op jit(solution)/shard_map/north/pallas_call | solution.py:566
  30.8 9.1 %shard_map.113 = (f32[53,3,24,128]{3,2,1,0:T(8,128)}, f32[4,3,8,128]{3,2,1,0:T(8,128)S(1)}) custom-call(s32[1]{0:T(128)} %bitcast.refs_0_, s32[3,1,24]{2,1,0:T(1,128)S(1)} %bitcast.12, f32[53,72,128]{2,1,0:T(8,128)S(1)} %get-tuple-element.20.refs_1_.refs_0_.refs_2_, f32[3816,128]{1,0:T(8,128)S(1)} %north.1.refs_3_, f32[3816,128]{1,0:T(8,128)S(1)} %upward.1.refs_4_, ...), custom_call_target="tpu_custom_call" | custom-call | flops 29306880 | bytes 1953792 | tf_op jit(solution)/shard_map/pallas_call | solution.py:588
  39.9 5.7 %shard_map.114 = (f32[53,3,24,128]{3,2,1,0:T(8,128)}, f32[3,8,128]{2,1,0:T(8,128)S(1)}, f32[3,8,128]{2,1,0:T(8,128)S(1)}, f32[3,8,128]{2,1,0:T(8,128)S(1)}, f32[3,8,128]{2,1,0:T(8,128)S(1)}) custom-call(s32[1]{0:T(128)} %bitcast.refs_0_, s32[3,1,24]{2,1,0:T(1,128)S(1)} %bitcast.13, ...), custom_call_target="tpu_custom_call", output_to_operand_aliasing={{0}: (14, {})} | custom-call | flops 29306880 | bytes 1953792 | tf_op jit(solution)/shard_map/pallas_call | solution.py:588
  45.5 0.1 collective-permute-start.7
  45.6 1.6 %collective-permute-start.8 = (f32[3,8,128]{2,1,0:T(8,128)S(1)}, f32[3,8,128]{2,1,0:T(8,128)S(1)}, u32[]{:S(2)}, u32[]{:S(2)}) collective-permute-start(f32[3,8,128]{2,1,0:T(8,128)S(1)} %get-tuple-element.36), channel_id=1, source_target_pairs={{0,16},{8,24},{16,0},{24,8},{1,17},{9,25},{17,1},{25,9},{2,18},{10... | collective-permute-start | bytes 36872 | tf_op jit(solution)/shard_map/ppermute | solution.py:19
  47.2 1.4 %collective-permute-start.9 = (f32[3,8,128]{2,1,0:T(8,128)S(1)}, f32[3,8,128]{2,1,0:T(8,128)S(1)}, u32[]{:S(2)}, u32[]{:S(2)}) collective-permute-start(f32[3,8,128]{2,1,0:T(8,128)S(1)} %get-tuple-element.37), channel_id=1, source_target_pairs={{0,24},{8,0},{16,8},{24,16},{1,25},{9,1},{17,9},{25,17},{2,26},{10... | collective-permute-start | bytes 36872 | tf_op jit(solution)/shard_map/ppermute | solution.py:19
  48.5 0.2 collective-permute-done.7.refs_1_
  48.7 0.7 %collective-permute-done.8.refs_2_ = f32[3,8,128]{2,1,0:T(8,128)S(1)} collective-permute-done((f32[3,8,128]{2,1,0:T(8,128)S(1)}, f32[3,8,128]{2,1,0:T(8,128)S(1)}, u32[]{:S(2)}, u32[]{:S(2)}) %collective-permute-start.8) | collective-permute-done | bytes 12320 | tf_op jit(solution)/shard_map/ppermute | solution.py:19
  49.4 0.6 %collective-permute-done.9.refs_3_ = f32[3,8,128]{2,1,0:T(8,128)S(1)} collective-permute-done((f32[3,8,128]{2,1,0:T(8,128)S(1)}, f32[3,8,128]{2,1,0:T(8,128)S(1)}, u32[]{:S(2)}, u32[]{:S(2)}) %collective-permute-start.9) | collective-permute-done | bytes 12320 | tf_op jit(solution)/shard_map/ppermute | solution.py:19
  50.0 1.0 %core.1 = f32[6,64,128]{2,1,0:T(8,128)} custom-call(f32[3,8,128]{2,1,0:T(8,128)S(1)} %get-tuple-element.34.refs_0_, f32[3,8,128]{2,1,0:T(8,128)S(1)} %collective-permute-done.7.refs_1_, f32[3,8,128]{2,1,0:T(8,128)S(1)} %collective-permute-done.8.refs_2_, f32[3,8,128]{2,1,0:T(8,128)S(1)} %collective-permute-done.9.refs_3_), custom_call_target="tpu_custom_call" | custom-call | tf_op jit(solution)/shard_map/core/pallas_call | solution.py:619
  (10 shorter events, 0.0 us)
Async XLA Ops:
  4.1 26.6 %collective-permute-start.6 = (bf16[53,3,16,128]{3,2,1,0:T(8,128)(2,1)}, bf16[53,3,16,128]{3,2,1,0:T(8,128)(2,1)S(1)}, u32[]{:S(2)}, u32[]{:S(2)}) collective-permute-start(bf16[53,3,16,128]{3,2,1,0:T(8,128)(2,1)} %get-tuple-element.30), channel_id=1, source_target_pairs={{8,16},{24,0},{16,8},{0,24},{9,17},{25,1},{17,9},{1,25},{10,18},{2... | collective-permute-start | bytes 1953800 | tf_op jit(solution)/shard_map/ppermute | solution.py:26
  6.6 24.2 %collective-permute-start.5 = (bf16[53,3,16,128]{3,2,1,0:T(8,128)(2,1)}, bf16[53,3,16,128]{3,2,1,0:T(8,128)(2,1)S(1)}, u32[]{:S(2)}, u32[]{:S(2)}) collective-permute-start(bf16[53,3,16,128]{3,2,1,0:T(8,128)(2,1)} %get-tuple-element.30), channel_id=1, source_target_pairs={{0,8},{16,24},{8,0},{24,16},{1,9},{17,25},{9,1},{25,17},{2,10},{18... | collective-permute-start | bytes 1953800 | tf_op jit(solution)/shard_map/ppermute | solution.py:26
  7.3 32.6 %collective-permute-start.4 = (bf16[53,3,8,128]{3,2,1,0:T(8,128)(2,1)}, bf16[53,3,8,128]{3,2,1,0:T(8,128)(2,1)}, u32[]{:S(2)}, u32[]{:S(2)}) collective-permute-start(bf16[53,3,8,128]{3,2,1,0:T(8,128)(2,1)} %get-tuple-element.25), channel_id=1, source_target_pairs={{8,16},{24,0},{16,8},{0,24},{9,17},{25,1},{17,9},{1,25},{10,18},{2... | collective-permute-start | bytes 976904 | tf_op jit(solution)/shard_map/ppermute | solution.py:26
  7.3 32.5 %collective-permute-start.3 = (bf16[53,3,8,128]{3,2,1,0:T(8,128)(2,1)}, bf16[53,3,8,128]{3,2,1,0:T(8,128)(2,1)}, u32[]{:S(2)}, u32[]{:S(2)}) collective-permute-start(bf16[53,3,8,128]{3,2,1,0:T(8,128)(2,1)} %get-tuple-element.25), channel_id=1, source_target_pairs={{0,8},{16,24},{8,0},{24,16},{1,9},{17,25},{9,1},{25,17},{2,10},{18... | collective-permute-start | bytes 976904 | tf_op jit(solution)/shard_map/ppermute | solution.py:26
  7.4 4.1 %collective-permute-start.2 = (bf16[192,128]{1,0:T(8,128)(2,1)S(1)}, bf16[192,128]{1,0:T(8,128)(2,1)S(1)}, u32[]{:S(2)}, u32[]{:S(2)}) collective-permute-start(bf16[192,128]{1,0:T(8,128)(2,1)S(1)} %get-tuple-element.24), channel_id=1, source_target_pairs={{0,1},{1,0},{2,3},{3,2},{4,5},{5,4},{6,7},{7,6},{8,9},{9,8},{10,11... | collective-permute-start | bytes 147464 | tf_op jit(solution)/shard_map/ppermute | solution.py:19
  11.5 5.0 %collective-permute-start = (bf16[9,56,128]{2,1,0:T(8,128)(2,1)S(1)}, bf16[9,56,128]{2,1,0:T(8,128)(2,1)S(1)}, u32[]{:S(2)}, u32[]{:S(2)}) collective-permute-start(bf16[9,56,128]{2,1,0:T(8,128)(2,1)S(1)} %get-tuple-element.21), channel_id=1, source_target_pairs={{0,2},{4,6},{2,0},{6,4},{1,3},{5,7},{3,1},{7,5},{8,10},{12,14},{10... | collective-permute-start | bytes 387080 | tf_op jit(solution)/shard_map/ppermute | solution.py:26
  16.5 0.7 %copy-start = (bf16[9,56,128]{2,1,0:T(8,128)(2,1)}, bf16[9,56,128]{2,1,0:T(8,128)(2,1)S(1)}, u32[]{:S(2)}) copy-start(bf16[9,56,128]{2,1,0:T(8,128)(2,1)S(1)} %collective-permute-done.refs_2_) | copy-start | bytes 387076
  17.2 8.8 %collective-permute-start.1 = (bf16[9,56,128]{2,1,0:T(8,128)(2,1)}, bf16[9,56,128]{2,1,0:T(8,128)(2,1)}, u32[]{:S(2)}, u32[]{:S(2)}) collective-permute-start(bf16[9,56,128]{2,1,0:T(8,128)(2,1)} %get-tuple-element.22), channel_id=1, source_target_pairs={{2,4},{6,0},{4,2},{0,6},{3,5},{7,1},{5,3},{1,7},{10,12},{14,8},{12... | collective-permute-start | bytes 387080 | tf_op jit(solution)/shard_map/ppermute | solution.py:26
  21.2 4.7 %copy-start.1 = (bf16[9,56,128]{2,1,0:T(8,128)(2,1)S(1)}, bf16[9,56,128]{2,1,0:T(8,128)(2,1)}, u32[]{:S(2)}) copy-start(bf16[9,56,128]{2,1,0:T(8,128)(2,1)} %copy-done) | copy-start | bytes 387076
  25.9 4.9 %copy-start.2 = (f32[3,64]{1,0:T(4,128)S(1)}, f32[3,64]{1,0:T(4,128)}, u32[]{:S(2)}) copy-start(f32[3,64]{1,0:T(4,128)} %refs_12_.3) | copy-start | bytes 2308
  25.9 4.9 %copy-start.3 = (s32[1,3,24,1]{2,3,1,0:T(1,128)S(1)}, s32[1,3,24,1]{2,3,1,0:T(1,128)}, u32[]{:S(2)}) copy-start(s32[1,3,24,1]{2,3,1,0:T(1,128)} %param.13) | copy-start | bytes 868
  45.5 3.2 %collective-permute-start.7 = (f32[3,8,128]{2,1,0:T(8,128)S(1)}, f32[3,8,128]{2,1,0:T(8,128)S(1)}, u32[]{:S(2)}, u32[]{:S(2)}) collective-permute-start(f32[3,8,128]{2,1,0:T(8,128)S(1)} %get-tuple-element.35), channel_id=1, source_target_pairs={{0,8},{8,16},{16,24},{24,0},{1,9},{9,17},{17,25},{25,1},{2,10},{10... | collective-permute-start | bytes 36872 | tf_op jit(solution)/shard_map/ppermute | solution.py:19
  45.6 3.8 %collective-permute-start.8 = (f32[3,8,128]{2,1,0:T(8,128)S(1)}, f32[3,8,128]{2,1,0:T(8,128)S(1)}, u32[]{:S(2)}, u32[]{:S(2)}) collective-permute-start(f32[3,8,128]{2,1,0:T(8,128)S(1)} %get-tuple-element.36), channel_id=1, source_target_pairs={{0,16},{8,24},{16,0},{24,8},{1,17},{9,25},{17,1},{25,9},{2,18},{10... | collective-permute-start | bytes 36872 | tf_op jit(solution)/shard_map/ppermute | solution.py:19
  47.2 2.8 %collective-permute-start.9 = (f32[3,8,128]{2,1,0:T(8,128)S(1)}, f32[3,8,128]{2,1,0:T(8,128)S(1)}, u32[]{:S(2)}, u32[]{:S(2)}) collective-permute-start(f32[3,8,128]{2,1,0:T(8,128)S(1)} %get-tuple-element.37), channel_id=1, source_target_pairs={{0,24},{8,0},{16,8},{24,16},{1,25},{9,1},{17,9},{25,17},{2,26},{10... | collective-permute-start | bytes 36872 | tf_op jit(solution)/shard_map/ppermute | solution.py:19
